TPU v7x, 32 devices: a 4x2x2 block of a 4x4x8 slice. The times are simulated.
32 devices in a mesh: data: 4 (over y, z), model: 8 (over x, core).
Axes of the slice: x: 4, y: 2, z: 2, core: 2. Of those that a mesh axis runs over, the one named last changes fastest.
The devices are a block of a 4x4x8 slice.
Arguments:
- tokens: bfloat16 [32, 512, 1024], P('data'), parts along dimension 0
- seg_ids: int32 [32, 512], P('data'), parts along dimension 0
- d_out: bfloat16 [32, 512, 1024], P('data'), parts along dimension 0
- gain_attn: bfloat16 [1024], replicated
- gain_mlp: bfloat16 [1024], replicated
- w_qkv: bfloat16 [1024, 16, 3, 64], P(None, 'model')
- w_out: bfloat16 [16, 64, 1024], P('model')
- w_up: bfloat16 [1024, 4096], P(None, 'model')
- w_down: bfloat16 [4096, 1024], P('model')
Outputs:
- output 1: bfloat16 [32, 512, 1024], P('data'), parts along dimension 0
- output 2: bfloat16 [32, 512, 1024], P('data'), parts along dimension 0
- output 3: bfloat16 [4096, 16, 3, 64], P('data', 'model'), parts along dimension 0
- output 4: bfloat16 [64, 64, 1024], P(('data', 'model')), parts along dimension 0
- output 5: bfloat16 [4096, 4096], P('data', 'model'), parts along dimension 0
- output 6: bfloat16 [16384, 1024], P(('data', 'model')), parts along dimension 0
- output 7: float32 [4096], P('data'), parts along dimension 0
- output 8: float32 [4096], P('data'), parts along dimension 0
There are 4 independent parts. A program takes and returns all parts, laid end to end along the dimension named above; an argument that names none is the same for every part.
All inputs are finite; a program needn't handle non-finite values.
Results may differ from a plain program's by a relative error of at most 0.02.
Values are sent between devices in bfloat16 or wider.
A program may use at most 768 MiB of HBM per device.

v0:
```python
import functools
import jax
import jax.numpy as jnp
from jax import lax
from jax.sharding import PartitionSpec as P

NORM_EPS = 1e-5


def layer_norm(values, gain_vec):
    mean_val = jnp.mean(values, axis=-1, keepdims=True)
    centered = values - mean_val
    var_val = jnp.mean(centered * centered, axis=-1, keepdims=True)
    return centered * lax.rsqrt(var_val + NORM_EPS) * gain_vec


def causal_mask(seg_ids):
    seq_len = seg_ids.shape[-1]
    query_pos = lax.broadcasted_iota(jnp.int32, (seq_len, seq_len), 0)
    key_pos = lax.broadcasted_iota(jnp.int32, (seq_len, seq_len), 1)
    same_doc = seg_ids[:, :, None] == seg_ids[:, None, :]
    return (same_doc & (query_pos >= key_pos)[None])[:, None]


def forward_pass(tokens, allowed, gain_attn, gain_mlp, w_qkv, w_out, w_up, w_down, reduce_sum):
    head_dim = w_qkv.shape[3]
    x_f32 = tokens.astype(jnp.float32)
    normed = layer_norm(x_f32, gain_attn.astype(jnp.float32)).astype(jnp.bfloat16)
    qkv_all = jnp.einsum('bsh,hnjd->jbnsd', normed, w_qkv, preferred_element_type=jnp.float32).astype(jnp.bfloat16)
    scores = jnp.einsum('bnqd,bnkd->bnqk', qkv_all[0], qkv_all[1], preferred_element_type=jnp.float32) * (head_dim ** -0.5)
    attn_probs = jax.nn.softmax(jnp.where(allowed, scores, -1e30), axis=-1)
    probs_bf = attn_probs.astype(jnp.bfloat16)
    attn_heads = jnp.einsum('bnqk,bnkd->bnqd', probs_bf, qkv_all[2], preferred_element_type=jnp.float32).astype(jnp.bfloat16)
    attn_proj = reduce_sum(jnp.einsum('bnsd,ndh->bsh', attn_heads, w_out, preferred_element_type=jnp.float32).astype(jnp.bfloat16))
    resid_f32 = (x_f32 + attn_proj.astype(jnp.float32)).astype(jnp.bfloat16).astype(jnp.float32)
    normed_mlp = layer_norm(resid_f32, gain_mlp.astype(jnp.float32)).astype(jnp.bfloat16)
    pre_act = jnp.einsum('bsh,hf->bsf', normed_mlp, w_up, preferred_element_type=jnp.float32)
    hidden = jax.nn.gelu(pre_act, approximate=True).astype(jnp.bfloat16)
    mlp_down = reduce_sum(jnp.einsum('bsf,fh->bsh', hidden, w_down, preferred_element_type=jnp.float32).astype(jnp.bfloat16))
    layer_out = (resid_f32 + mlp_down.astype(jnp.float32)).astype(jnp.bfloat16)
    saved = dict(normed=normed, qkv_all=qkv_all, attn_probs=attn_probs, probs_bf=probs_bf, attn_heads=attn_heads, resid_f32=resid_f32, normed_mlp=normed_mlp, pre_act=pre_act, hidden=hidden)
    return layer_out, saved


def backward_pass(tokens, d_out, gain_attn, gain_mlp, w_qkv, w_out, w_up, w_down, saved, reduce_sum):
    head_dim = w_qkv.shape[3]
    qkv_all = saved['qkv_all']
    attn_probs = saved['attn_probs']
    d_hidden = jnp.einsum('bsh,fh->bsf', d_out, w_down, preferred_element_type=jnp.float32).astype(jnp.bfloat16)
    d_w_down = jnp.einsum('bsf,bsh->fh', saved['hidden'], d_out, preferred_element_type=jnp.float32).astype(jnp.bfloat16)
    _, gelu_back = jax.vjp(functools.partial(jax.nn.gelu, approximate=True), saved['pre_act'])
    d_pre = gelu_back(d_hidden.astype(jnp.float32))[0].astype(jnp.bfloat16)
    d_normed_mlp = reduce_sum(jnp.einsum('bsf,hf->bsh', d_pre, w_up, preferred_element_type=jnp.float32).astype(jnp.bfloat16))
    d_w_up = jnp.einsum('bsh,bsf->hf', saved['normed_mlp'], d_pre, preferred_element_type=jnp.float32).astype(jnp.bfloat16)
    _, norm_mlp_back = jax.vjp(layer_norm, saved['resid_f32'], gain_mlp.astype(jnp.float32))
    d_resid_norm, d_gain_mlp = norm_mlp_back(d_normed_mlp.astype(jnp.float32))
    d_resid = (d_out.astype(jnp.float32) + d_resid_norm).astype(jnp.bfloat16)
    d_heads = jnp.einsum('bsh,ndh->bnsd', d_resid, w_out, preferred_element_type=jnp.float32).astype(jnp.bfloat16)
    d_w_out = jnp.einsum('bnsd,bsh->ndh', saved['attn_heads'], d_resid, preferred_element_type=jnp.float32).astype(jnp.bfloat16)
    d_probs = jnp.einsum('bnqd,bnkd->bnqk', d_heads, qkv_all[2], preferred_element_type=jnp.float32)
    d_value = jnp.einsum('bnqk,bnqd->bnkd', saved['probs_bf'], d_heads, preferred_element_type=jnp.float32).astype(jnp.bfloat16)
    row_dot = jnp.sum(d_probs * attn_probs, axis=-1, keepdims=True)
    d_scores = (attn_probs * (d_probs - row_dot) * (head_dim ** -0.5)).astype(jnp.bfloat16)
    d_query = jnp.einsum('bnqk,bnkd->bnqd', d_scores, qkv_all[1], preferred_element_type=jnp.float32).astype(jnp.bfloat16)
    d_key = jnp.einsum('bnqk,bnqd->bnkd', d_scores, qkv_all[0], preferred_element_type=jnp.float32).astype(jnp.bfloat16)
    d_qkv = jnp.stack([d_query, d_key, d_value])
    d_normed = reduce_sum(jnp.einsum('jbnsd,hnjd->bsh', d_qkv, w_qkv, preferred_element_type=jnp.float32).astype(jnp.bfloat16))
    d_w_qkv = jnp.einsum('bsh,jbnsd->hnjd', saved['normed'], d_qkv, preferred_element_type=jnp.float32).astype(jnp.bfloat16)
    _, norm_attn_back = jax.vjp(layer_norm, tokens.astype(jnp.float32), gain_attn.astype(jnp.float32))
    d_x_norm, d_gain_attn = norm_attn_back(d_normed.astype(jnp.float32))
    d_tokens = (d_resid.astype(jnp.float32) + d_x_norm).astype(jnp.bfloat16)
    return (d_tokens, d_w_qkv, d_w_out, d_w_up, d_w_down, d_gain_attn, d_gain_mlp)


def solution(mesh):
    reduce_sum = functools.partial(lax.psum, axis_name='model')

    def device_step(tokens, seg_ids, d_out, gain_attn, gain_mlp, w_qkv, w_out, w_up, w_down):
        allowed = causal_mask(seg_ids)
        layer_out, _ = forward_pass(tokens, allowed, gain_attn, gain_mlp, w_qkv, w_out, w_up, w_down, reduce_sum)
        tokens_again = lax.optimization_barrier((tokens, layer_out))[0]
        _, saved = forward_pass(tokens_again, allowed, gain_attn, gain_mlp, w_qkv, w_out, w_up, w_down, reduce_sum)
        grad_list = backward_pass(tokens_again, d_out, gain_attn, gain_mlp, w_qkv, w_out, w_up, w_down, saved, reduce_sum)
        return (layer_out,) + grad_list

    in_specs = (P('data', None, None), P('data', None), P('data', None, None), P(), P(), P(None, 'model', None, None), P('model', None, None), P(None, 'model'), P('model', None))
    out_specs = (P('data', None, None), P('data', None, None), P('data', 'model', None, None), P(('data', 'model'), None, None), P('data', 'model'), P(('data', 'model'), None), P('data'), P('data'))
    return jax.shard_map(device_step, mesh=mesh, in_specs=in_specs, out_specs=out_specs, check_vma=False)
```

profile of v0, /device:TPU:81, one launch (start us, length us, event | category | flops | bytes accessed | tf_op | source)
XLA Modules:
  0.0 802.1 jit_solution(5117861165909476375)
XLA Ops:
  17.8 5.9 convert_bitcast_fusion.1
  23.7 11.3 %fusion.196 = (f32[8,2,512]{2,1,0:T(2,128)S(1)}, f32[8,2,512,512]{2,3,1,0:T(8,128)}) fusion(pred[8,512,512]{1,2,0:T(8,128)(4,1)S(1)} %compare_and_fusion, bf16[3,8,2,512,64]{3,4,0,2,1:T(8,128)(2,1)} %convert_bitcast_fusion.1), kind=kOutput, calls=%fused_computation.206 | convolution fusion | flops 553648640 | bytes 21004288 | tf_op jit(solution)/shard_map/sub | solution.py:31
  35.0 10.1 %bitcast_convert_fusion.2 = bf16[8,512,1024]{2,1,0:T(8,128)(2,1)} fusion(f32[8,2,512,512]{2,3,1,0:T(8,128)} %get-tuple-element.27, f32[8,2,512]{2,1,0:T(2,128)S(1)} %get-tuple-element.26, bf16[3,8,2,512,64]{3,4,0,2,1:T(8,128)(2,1)} %convert_bitcast_fusion.1, bf16[2,64,1024]{2,1,0:T(8,128)(2,1)S(1)} %copy-done.12), kind=kOutput, calls=%fused_computation.55 | convolution fusion | flops 1623719936 | bytes 26509312 | tf_op jit(solution)/shard_map/bnsd,ndh->bsh/dot_general | solution.py:34
  45.8 101.1 %all-reduce.6.cloned.1.call-done = bf16[8,512,1024]{2,1,0:T(8,128)(2,1)} async-done(((bf16[8,512,1024]{2,1,0:T(8,128)(2,1)}), bf16[8,512,1024]{2,1,0:T(8,128)(2,1)}) %all-reduce.6.cloned.1.call-update) | async-done | bytes 8388624 | tf_op jit(solution)/shard_map/psum | solution.py:34
  146.9 7.3 convert_reduce_fusion.1
  160.4 14.0 %convolution_convert_fusion.1 = bf16[8,512,1024]{2,1,0:T(8,128)(2,1)} fusion(bf16[8,512,1024]{2,1,0:T(8,128)(2,1)} %copy-done.7, f32[1024]{0:T(1024)S(1)} %convert_element_type.169, f32[8,512]{1,0:T(8,128)S(1)} %add_rsqrt_fusion, f32[8,512]{1,0:T(8,128)S(1)} %broadcast_multiply_fusion.2, bf16[512,1024]{1,0:T(8,128)(2,1)} %param.17, ...), kind=kOutput, calls=%fused_computation.120 | convolution fusion | flops 8633974784 | bytes 18911232 | tf_op jit(solution)/shard_map/bsf,fh->bsh/dot_general | solution.py:39
  174.6 97.7 %all-reduce.8.cloned.1.call-done = bf16[8,512,1024]{2,1,0:T(8,128)(2,1)} async-done(((bf16[8,512,1024]{2,1,0:T(8,128)(2,1)}), bf16[8,512,1024]{2,1,0:T(8,128)(2,1)}) %all-reduce.8.cloned.1.call-update) | async-done | bytes 8388624 | tf_op jit(solution)/shard_map/psum | solution.py:39
  272.2 10.6 %fusion.32 = bf16[8,512,1024]{2,1,0:T(8,128)(2,1)} fusion(bf16[8,512,1024]{2,1,0:T(8,128)(2,1)} %copy-done.7, bf16[8,512,1024]{2,1,0:T(8,128)(2,1)} %all-reduce.8.cloned.1.call-done), kind=kLoop, calls=%fused_computation.49 | loop fusion | flops 16777216 | bytes 25165824 | tf_op jit(solution)/shard_map/convert_element_type | solution.py:40
  294.5 5.9 convert_bitcast_fusion
  300.4 11.2 %fusion.197 = (f32[8,2,512]{2,1,0:T(2,128)S(1)}, f32[8,2,512,512]{2,3,1,0:T(8,128)}) fusion(pred[8,512,512]{1,2,0:T(8,128)(4,1)S(1)} %compare_and_fusion, bf16[3,8,2,512,64]{3,4,0,2,1:T(8,128)(2,1)} %convert_bitcast_fusion), kind=kOutput, calls=%fused_computation.207 | convolution fusion | flops 553648640 | bytes 21004288 | tf_op jit(solution)/shard_map/sub | solution.py:31
  311.6 7.7 fusion.124
  320.3 5.8 bitcast_convert_fusion.1
  326.6 97.2 %all-reduce.10.cloned.1.call-done = bf16[8,512,1024]{2,1,0:T(8,128)(2,1)} async-done(((bf16[8,512,1024]{2,1,0:T(8,128)(2,1)}), bf16[8,512,1024]{2,1,0:T(8,128)(2,1)}) %all-reduce.10.cloned.1.call-update) | async-done | bytes 8388624 | tf_op jit(solution)/shard_map/psum | solution.py:34
  423.8 7.3 convert_reduce_fusion.3
  440.8 10.5 %fusion.45 = bf16[8,512,512]{2,1,0:T(8,128)(2,1)} fusion(f32[8,512,512]{2,1,0:T(8,128)S(1)} %fusion.92, bf16[8,512,1024]{2,1,0:T(8,128)(2,1)S(1)} %bitcast.180, bf16[512,1024]{1,0:T(8,128)(2,1)S(1)} %copy-done.21), kind=kOutput, calls=%fused_computation.77 | convolution fusion | flops 4341104640 | bytes 22020096 | tf_op jit(solution)/shard_map/bsh,fh->bsf/dot_general | solution.py:49
  451.3 9.0 %convolution_convert_fusion = bf16[8,512,1024]{2,1,0:T(8,128)(2,1)} fusion(bf16[8,512,512]{2,1,0:T(8,128)(2,1)} %fusion.45, bf16[1024,512]{1,0:T(8,128)(2,1)S(1)} %copy-done), kind=kOutput, calls=%fused_computation.119 | convolution fusion | flops 4299161600 | bytes 13631488 | tf_op jit(solution)/shard_map/bsf,hf->bsh/dot_general | solution.py:53
  460.6 97.5 %all-reduce.12.cloned.1.call-done = bf16[8,512,1024]{2,1,0:T(8,128)(2,1)} async-done(((bf16[8,512,1024]{2,1,0:T(8,128)(2,1)}), bf16[8,512,1024]{2,1,0:T(8,128)(2,1)}) %all-reduce.12.cloned.1.call-update) | async-done | bytes 8388624 | tf_op jit(solution)/shard_map/psum | solution.py:53
  558.1 8.7 %fusion.28 = f32[8,512]{1,0:T(8,128)S(1)} fusion(bf16[8,512,1024]{2,1,0:T(8,128)(2,1)} %all-reduce.12.cloned.1.call-done, bf16[8,512,1024]{2,1,0:T(8,128)(2,1)} %copy-done.3, f32[8,512]{1,0:T(8,128)S(1)} %broadcast_multiply_fusion, f32[1024]{0:T(1024)S(1)} %convert_element_type.169), kind=kLoop, calls=%fused_computation.45 | loop fusion | flops 25161728 | bytes 16814080 | tf_op jit(solution)/shard_map/transpose(jvp())/reduce_sum | solution.py:14
  566.8 12.6 %fusion.29 = (f32[1024]{0:T(1024)}, f32[8,512]{1,0:T(8,128)S(1)}) fusion(bf16[8,512,1024]{2,1,0:T(8,128)(2,1)S(1)} %copy-done.6, bf16[8,512,1024]{2,1,0:T(8,128)(2,1)} %copy-done.3, f32[8,512]{1,0:T(8,128)S(1)} %fusion.173, f32[8,512]{1,0:T(8,128)S(1)} %broadcast_multiply_fusion, f32[8,512]{1,0:T(8,128)S(1)} %multiply_multiply_fusion.4, ...), kind=kLoop, calls=%fused_computation.46 | loop fusion | flops 50326528 | bytes 16850944 | tf_op jit(solution)/shard_map/transpose(jvp())/reduce_sum | solution.py:14
  579.5 8.9 %add_convert_fusion.1 = bf16[8,512,1024]{2,1,0:T(8,128)(2,1)S(1)} fusion(bf16[8,512,1024]{2,1,0:T(8,128)(2,1)} %param.11, bf16[8,512,1024]{2,1,0:T(8,128)(2,1)S(1)} %bitcast.174, bf16[8,512,1024]{2,1,0:T(8,128)(2,1)S(1)} %copy-done.6, f32[8,512]{1,0:T(8,128)S(1)} %negate_multiply_fusion.1, f32[8,512]{1,0:T(8,128)S(1)} %multiply_multiply_fusion.4, ...), kind=kLoop, calls=%fused_computation.60 | loop fusion | flops 50331648 | bytes 33624064 | tf_op jit(solution)/shard_map/convert_element_type | solution.py:57
  594.5 8.4 %fusion.147 = bf16[1,8,2,512,64]{3,4,2,1,0:T(8,128)(2,1)S(1)} fusion(bf16[8,2,512,64]{2,3,1,0:T(8,128)(2,1)S(1)} %fusion.138, f32[8,2,512,512]{2,3,1,0:T(8,128)} %get-tuple-element.29, f32[8,2,512]{2,1,0:T(2,128)S(1)} %get-tuple-element.28), kind=kOutput, calls=%fused_computation.149 | convolution fusion | flops 545783808 | bytes 18907136 | tf_op jit(solution)/shard_map/bnqk,bnqd->bnkd/dot_general | solution.py:61
  603.0 9.3 %fusion.166 = f32[8,2,512,512]{2,3,1,0:T(8,128)} fusion(bf16[8,2,512,64]{2,3,1,0:T(8,128)(2,1)S(1)} %fusion.138, bf16[3,8,2,512,64]{3,4,0,2,1:T(8,128)(2,1)} %convert_bitcast_fusion), kind=kOutput, calls=%fused_computation.166 | convolution fusion | flops 536870912 | bytes 18874368 | tf_op jit(solution)/shard_map/bnqd,bnkd->bnqk/dot_general | solution.py:60
  612.3 22.4 %fusion.144 = bf16[1,8,2,512,64]{3,4,2,1,0:T(8,128)(2,1)S(1)} fusion(f32[8,2,512,512]{2,3,1,0:T(8,128)} %fusion.166, bf16[3,8,2,512,64]{3,4,0,2,1:T(8,128)(2,1)} %convert_bitcast_fusion, f32[8,2,512,512]{2,3,1,0:T(8,128)} %get-tuple-element.29, f32[8,2,512]{2,1,0:T(2,128)S(1)} %get-tuple-element.28), kind=kOutput, calls=%fused_computation.148 | convolution fusion | flops 566764032 | bytes 69271552 | tf_op jit(solution)/shard_map/bnqk,bnkd->bnqd/dot_general | solution.py:64
  634.7 23.6 %fusion.141 = bf16[1,8,2,512,64]{3,4,2,1,0:T(8,128)(2,1)} fusion(f32[8,2,512,512]{2,3,1,0:T(8,128)} %fusion.166, bf16[3,8,2,512,64]{3,4,0,2,1:T(8,128)(2,1)} %convert_bitcast_fusion, f32[8,2,512,512]{2,3,1,0:T(8,128)} %get-tuple-element.29, f32[8,2,512]{2,1,0:T(2,128)S(1)} %get-tuple-element.28), kind=kOutput, calls=%fused_computation.147 | convolution fusion | flops 566764032 | bytes 69271552 | tf_op jit(solution)/shard_map/bnqk,bnqd->bnkd/dot_general | solution.py:65
  658.3 8.3 %bitcast_convert_fusion = bf16[8,512,1024]{2,1,0:T(8,128)(2,1)} fusion(bf16[1,8,2,512,64]{3,4,2,1,0:T(8,128)(2,1)S(1)} %fusion.147, bf16[1,8,2,512,64]{3,4,2,1,0:T(8,128)(2,1)} %fusion.141, bf16[1,8,2,512,64]{3,4,2,1,0:T(8,128)(2,1)S(1)} %fusion.144, bf16[1024,2,3,64]{0,3,2,1:T(8,128)(2,1)S(1)} %copy-done.24), kind=kOutput, calls=%fused_computation.53 | convolution fusion | flops 3228565504 | bytes 12320768 | tf_op jit(solution)/shard_map/jbnsd,hnjd->bsh/dot_general | solution.py:67
  666.7 11.6 %bitcast_convert_fusion.3 = bf16[512,1024]{1,0:T(8,128)(2,1)} fusion(bf16[8,512,1024]{2,1,0:T(8,128)(2,1)} %param.11, f32[8,512,512]{2,1,0:T(8,128)} %copy-done.25), kind=kOutput, calls=%fused_computation.135 | convolution fusion | flops 4314365952 | bytes 17825792 | tf_op jit(solution)/shard_map/bsf,bsh->fh/dot_general | solution.py:50
  678.2 9.4 %bitcast_convert_fusion.4 = bf16[1024,512]{1,0:T(8,128)(2,1)} fusion(bf16[8,512,512]{2,1,0:T(8,128)(2,1)S(1)} %copy-done.26, bf16[8,512,1024]{2,1,0:T(8,128)(2,1)} %copy-done.3, f32[8,512]{1,0:T(8,128)S(1)} %fusion.173, f32[8,512]{1,0:T(8,128)S(1)} %broadcast_multiply_fusion, f32[1024]{0:T(1024)S(1)} %convert_element_type.169), kind=kOutput, calls=%fused_computation.136 | convolution fusion | flops 4316463104 | bytes 13668352 | tf_op jit(solution)/shard_map/bsh,bsf->hf/dot_general | solution.py:54
  687.7 7.4 fusion.150
  698.1 66.3 %all-reduce.14.cloned.1.call-done = bf16[8,512,1024]{2,1,0:T(8,128)(2,1)} async-done(((bf16[8,512,1024]{2,1,0:T(8,128)(2,1)}), bf16[8,512,1024]{2,1,0:T(8,128)(2,1)}) %all-reduce.14.cloned.1.call-update) | async-done | bytes 8388624 | tf_op jit(solution)/shard_map/psum | solution.py:67
  764.4 8.7 %fusion.34 = f32[8,512]{1,0:T(8,128)S(1)} fusion(bf16[8,512,1024]{2,1,0:T(8,128)(2,1)} %all-reduce.14.cloned.1.call-done, bf16[8,512,1024]{2,1,0:T(8,128)(2,1)} %param.9, f32[8,512]{1,0:T(8,128)S(1)} %copy-done.11, f32[1024]{0:T(1024)S(1)} %copy-done.19), kind=kLoop, calls=%fused_computation.51 | loop fusion | flops 25161728 | bytes 16814080 | tf_op jit(solution)/shard_map/transpose(jvp())/reduce_sum | solution.py:14
  773.1 13.3 %fusion.30 = (f32[1024]{0:T(1024)}, f32[8,512]{1,0:T(8,128)S(1)}) fusion(bf16[8,512,1024]{2,1,0:T(8,128)(2,1)S(1)} %copy-done.5, bf16[8,512,1024]{2,1,0:T(8,128)(2,1)} %param.9, f32[8,512]{1,0:T(8,128)S(1)} %copy-done.16, f32[8,512]{1,0:T(8,128)S(1)} %copy-done.11, f32[8,512]{1,0:T(8,128)S(1)} %multiply_multiply_fusion.3, f32[1024]{0:T(1024)S(1)} %copy-done.19), kind=kLoop, calls=%fused_computation.47 | loop fusion | flops 50326528 | bytes 16850944 | tf_op jit(solution)/shard_map/transpose(jvp())/reduce_sum | solution.py:14
  786.5 8.6 %add_convert_fusion = bf16[8,512,1024]{2,1,0:T(8,128)(2,1)} fusion(bf16[8,512,1024]{2,1,0:T(8,128)(2,1)S(1)} %bitcast.178, bf16[8,512,1024]{2,1,0:T(8,128)(2,1)S(1)} %bitcast.172, bf16[8,512,1024]{2,1,0:T(8,128)(2,1)S(1)} %copy-done.5, f32[8,512]{1,0:T(8,128)S(1)} %negate_multiply_fusion, f32[8,512]{1,0:T(8,128)S(1)} %multiply_multiply_fusion.3, ...), kind=kLoop, calls=%fused_computation.56 | loop fusion | flops 50331648 | bytes 33624064 | tf_op jit(solution)/shard_map/convert_element_type | solution.py:71
  (122 shorter events, 49.7 us)
Async XLA Ops:
  7.2 153.2 %copy-start = (bf16[1024,512]{1,0:T(8,128)(2,1)S(1)}, bf16[1024,512]{1,0:T(8,128)(2,1)}, u32[]{:S(2)}) copy-start(bf16[1024,512]{1,0:T(8,128)(2,1)} %param.16) | copy-start | bytes 3145732
  7.2 139.7 %all-reduce.6.cloned.1.call-start = ((), (), s32[]{:S(2)}) async-start(), calls=%async_computation | async-start | bytes 16777216 | tf_op jit(solution)/shard_map/psum | solution.py:34
  8.2 285.6 %copy-start.18 = (f32[1024]{0:T(1024)}, f32[1024]{0:T(1024)S(1)}, u32[]{:S(2)}) copy-start(f32[1024]{0:T(1024)S(1)} %convert_element_type.159) | copy-start | bytes 12292
  8.2 9.6 %copy-start.22 = (bf16[1024,2,3,64]{0,3,2,1:T(8,128)(2,1)S(1)}, bf16[1024,2,3,64]{0,3,2,1:T(8,128)(2,1)}, u32[]{:S(2)}) copy-start(bf16[1024,2,3,64]{0,3,2,1:T(8,128)(2,1)} %param.14) | copy-start | bytes 2359300
  23.7 11.3 %copy-start.12 = (bf16[2,64,1024]{2,1,0:T(8,128)(2,1)S(1)}, bf16[2,64,1024]{2,1,0:T(8,128)(2,1)}, u32[]{:S(2)}) copy-start(bf16[2,64,1024]{2,1,0:T(8,128)(2,1)} %param.15) | copy-start | bytes 786436
  45.1 227.1 %all-reduce.8.cloned.1.call-start = ((), (), s32[]{:S(2)}) async-start(), calls=%async_computation.1 | async-start | bytes 16777216 | tf_op jit(solution)/shard_map/psum | solution.py:39
  174.5 249.3 %all-reduce.10.cloned.1.call-start = ((), (), s32[]{:S(2)}) async-start(), calls=%async_computation.2 | async-start | bytes 16777216 | tf_op jit(solution)/shard_map/psum | solution.py:34
  282.9 11.6 %slice-start = ((s8[8388608]{0:T(1024)(128)(4,1)}), s8[4194304]{0:T(1024)(128)(4,1)S(1)}, s32[]{:S(2)}) async-start(s8[8388608]{0:T(1024)(128)(4,1)} %bitcast.169), calls=%async_computation.5 | async-start | bytes 8388608
  282.9 11.6 %copy-start.23 = (bf16[1024,2,3,64]{0,3,2,1:T(8,128)(2,1)S(1)}, bf16[1024,2,3,64]{0,3,2,1:T(8,128)(2,1)}, u32[]{:S(2)}) copy-start(bf16[1024,2,3,64]{0,3,2,1:T(8,128)(2,1)} %param.14) | copy-start | bytes 2359300
  326.1 232.0 %all-reduce.12.cloned.1.call-start = ((), (), s32[]{:S(2)}) async-start(), calls=%async_computation.3 | async-start | bytes 16777216 | tf_op jit(solution)/shard_map/psum | solution.py:53
  431.2 9.6 %slice-start.10 = ((s8[8388608]{0:T(1024)(128)(4,1)}), s8[4194304]{0:T(1024)(128)(4,1)S(1)}, s32[]{:S(2)}) async-start(s8[8388608]{0:T(1024)(128)(4,1)} %bitcast.179), calls=%async_computation.15 | async-start | bytes 8388608
  440.8 10.5 %copy-start.25 = (f32[8,512,512]{2,1,0:T(8,128)}, f32[8,512,512]{2,1,0:T(8,128)S(1)}, u32[]{:S(2)}) copy-start(f32[8,512,512]{2,1,0:T(8,128)S(1)} %fusion.92) | copy-start | bytes 25165828
  460.4 304.0 %all-reduce.14.cloned.1.call-start = ((), (), s32[]{:S(2)}) async-start(), calls=%async_computation.4 | async-start | bytes 16777216 | tf_op jit(solution)/shard_map/psum | solution.py:67
  558.1 8.7 %copy-start.6 = (bf16[8,512,1024]{2,1,0:T(8,128)(2,1)S(1)}, bf16[8,512,1024]{2,1,0:T(8,128)(2,1)}, u32[]{:S(2)}) copy-start(bf16[8,512,1024]{2,1,0:T(8,128)(2,1)} %all-reduce.12.cloned.1.call-done) | copy-start | bytes 25165828
  558.1 21.4 %slice-start.4 = ((s8[8388608]{0:T(1024)(128)(4,1)}), s8[4194304]{0:T(1024)(128)(4,1)S(1)}, s32[]{:S(2)}) async-start(s8[8388608]{0:T(1024)(128)(4,1)} %bitcast.173), calls=%async_computation.9 | async-start | bytes 8388608
  566.8 12.7 %slice-start.5 = ((s8[8388608]{0:T(1024)(128)(4,1)}), s8[4194304]{0:T(1024)(128)(4,1)S(1)}, s32[]{:S(2)}) async-start(s8[8388608]{0:T(1024)(128)(4,1)} %bitcast.173), calls=%async_computation.10 | async-start | bytes 8388608
  634.7 23.6 %copy-start.24 = (bf16[1024,2,3,64]{0,3,2,1:T(8,128)(2,1)S(1)}, bf16[1024,2,3,64]{0,3,2,1:T(8,128)(2,1)}, u32[]{:S(2)}) copy-start(bf16[1024,2,3,64]{0,3,2,1:T(8,128)(2,1)} %param.14) | copy-start | bytes 2359300
  666.6 11.6 %copy-start.26 = (bf16[8,512,512]{2,1,0:T(8,128)(2,1)S(1)}, bf16[8,512,512]{2,1,0:T(8,128)(2,1)}, u32[]{:S(2)}) copy-start(bf16[8,512,512]{2,1,0:T(8,128)(2,1)} %fusion.45) | copy-start | bytes 12582916
  678.2 9.4 %copy-start.11 = (f32[8,512]{1,0:T(8,128)S(1)}, f32[8,512]{1,0:T(8,128)}, u32[]{:S(2)}) copy-start(f32[8,512]{1,0:T(8,128)} %copy-done.10) | copy-start | bytes 49156
  678.2 9.4 %copy-start.16 = (f32[8,512]{1,0:T(8,128)S(1)}, f32[8,512]{1,0:T(8,128)}, u32[]{:S(2)}) copy-start(f32[8,512]{1,0:T(8,128)} %copy-done.15) | copy-start | bytes 49156
  678.2 9.4 %copy-start.19 = (f32[1024]{0:T(1024)S(1)}, f32[1024]{0:T(1024)}, u32[]{:S(2)}) copy-start(f32[1024]{0:T(1024)} %copy-done.18) | copy-start | bytes 12292
  678.2 9.4 %copy-start.27 = (bf16[1,8,2,512,64]{3,4,2,1,0:T(8,128)(2,1)S(1)}, bf16[1,8,2,512,64]{3,4,2,1,0:T(8,128)(2,1)}, u32[]{:S(2)}) copy-start(bf16[1,8,2,512,64]{3,4,2,1,0:T(8,128)(2,1)} %fusion.141) | copy-start | bytes 3145732
  678.2 17.8 %slice-start.6 = ((s8[8388608]{0:T(1024)(128)(4,1)}), s8[4194304]{0:T(1024)(128)(4,1)S(1)}, s32[]{:S(2)}) async-start(s8[8388608]{0:T(1024)(128)(4,1)} %bitcast.175), calls=%async_computation.11 | async-start | bytes 8388608
  687.6 8.4 %slice-start.7 = ((s8[8388608]{0:T(1024)(128)(4,1)}), s8[4194304]{0:T(1024)(128)(4,1)S(1)}, s32[]{:S(2)}) async-start(s8[8388608]{0:T(1024)(128)(4,1)} %bitcast.175), calls=%async_computation.12 | async-start | bytes 8388608
  687.7 8.4 %copy-start.9 = (bf16[8,2,512,64]{2,3,1,0:T(8,128)(2,1)S(1)}, bf16[8,2,512,64]{2,3,1,0:T(8,128)(2,1)}, u32[]{:S(2)}) copy-start(bf16[8,2,512,64]{2,3,1,0:T(8,128)(2,1)} %copy-done.8) | copy-start | bytes 3145732
  698.1 75.0 %copy-start.14 = (f32[8,512]{1,0:T(8,128)S(1)}, f32[8,512]{1,0:T(8,128)}, u32[]{:S(2)}) copy-start(f32[8,512]{1,0:T(8,128)} %copy-done.13) | copy-start | bytes 49156
  764.4 8.7 %copy-start.5 = (bf16[8,512,1024]{2,1,0:T(8,128)(2,1)S(1)}, bf16[8,512,1024]{2,1,0:T(8,128)(2,1)}, u32[]{:S(2)}) copy-start(bf16[8,512,1024]{2,1,0:T(8,128)(2,1)} %all-reduce.14.cloned.1.call-done) | copy-start | bytes 25165828
  764.4 22.1 %slice-start.2 = ((s8[8388608]{0:T(1024)(128)(4,1)}), s8[4194304]{0:T(1024)(128)(4,1)S(1)}, s32[]{:S(2)}) async-start(s8[8388608]{0:T(1024)(128)(4,1)} %bitcast.171), calls=%async_computation.7 | async-start | bytes 8388608
  764.4 22.1 %slice-start.8 = ((s8[8388608]{0:T(1024)(128)(4,1)}), s8[4194304]{0:T(1024)(128)(4,1)S(1)}, s32[]{:S(2)}) async-start(s8[8388608]{0:T(1024)(128)(4,1)} %bitcast.177), calls=%async_computation.13 | async-start | bytes 8388608
  773.1 13.3 %slice-start.3 = ((s8[8388608]{0:T(1024)(128)(4,1)}), s8[4194304]{0:T(1024)(128)(4,1)S(1)}, s32[]{:S(2)}) async-start(s8[8388608]{0:T(1024)(128)(4,1)} %bitcast.171), calls=%async_computation.8 | async-start | bytes 8388608
  773.1 13.3 %slice-start.9 = ((s8[8388608]{0:T(1024)(128)(4,1)}), s8[4194304]{0:T(1024)(128)(4,1)S(1)}, s32[]{:S(2)}) async-start(s8[8388608]{0:T(1024)(128)(4,1)} %bitcast.177), calls=%async_computation.14 | async-start | bytes 8388608
  786.5 8.7 %copy-start.1 = (bf16[1024,512]{1,0:T(8,128)(2,1)S(1)}, bf16[1024,512]{1,0:T(8,128)(2,1)}, u32[]{:S(2)}) copy-start(bf16[1024,512]{1,0:T(8,128)(2,1)} %param.16) | copy-start | bytes 3145732
  (13 other events, 51.5 us)
Sparse Core Ops, SparseCore 0:
  45.3 101.5 all-reduce.5
  174.6 97.5 all-reduce.7
  326.2 97.5 all-reduce.9
  460.5 97.5 all-reduce.11
  666.8 97.5 all-reduce.13
where the time goes:
time: 809 us; the launch traced here: 802 us
  waiting for transfers between devices  460 us (57%)
  matrix products  202 us (25%)
  other arithmetic  113 us (14%)
  between operations  14.9 us (2%)
  local copies, waits for them, and re-layouts  11.6 us (1%)
    psum x2, waiting for transfers between devices, forward_pass(): reduce_sum(jnp.einsum('bnsd,ndh->bsh', attn_heads, w_out, preferred_eleme...  198 us
    psum x1, waiting for transfers between devices, forward_pass(): reduce_sum(jnp.einsum('bsf,fh->bsh', hidden, w_down, preferred_element_ty...  97.7 us
    psum x1, waiting for transfers between devices, backward_pass(): reduce_sum(jnp.einsum('bsf,hf->bsh', d_pre, w_up, preferred_element_type=...  97.5 us
    psum x1, waiting for transfers between devices, backward_pass(): reduce_sum(jnp.einsum('jbnsd,hnjd->bsh', d_qkv, w_qkv, preferred_element_...  66.3 us
    reduce_sum x4, other arithmetic, layer_norm(): return centered * lax.rsqrt(var_val + NORM_EPS) * gain_vec  43.3 us
    reduce_sum x4, other arithmetic, layer_norm(): mean_val = jnp.mean(values, axis=-1, keepdims=True)  24.3 us
    dot_general x1, matrix products, backward_pass(): jnp.einsum('bnqk,bnqd->bnkd', d_scores, qkv_all[0], preferred_element_typ...  23.6 us
    sub x2, matrix products, forward_pass(): attn_probs = jax.nn.softmax(jnp.where(allowed, scores, -1e+30), axis=-1)  22.5 us
  transfers between devices with their start and end apart: 5, of which 5 were waited for; matrix products, arithmetic and copies ran while one was open for 4% of the time, Pallas kernels for 0%

commit v1 on v0

v1 whole, which is shorter than its diff:
```python
import functools
import jax
import jax.numpy as jnp
from jax import lax
from jax.experimental import pallas as pl
from jax.experimental.pallas import tpu as pltpu
from jax.sharding import PartitionSpec as P

NORM_EPS = 1e-5
MESH = pl.DeviceIdType.MESH
F32 = jnp.float32
BF16 = jnp.bfloat16
SLOTS = 4
BLOCKS = 16
HALF = BLOCKS // 2
PIECE = 2
COPIES = 13
VMEM_LIMIT = 66 * 1000 * 1000


def mm(a, b):
    return lax.dot_general(a, b, (((1,), (0,)), ((), ())), preferred_element_type=F32)


def mt(a, b):
    return lax.dot_general(a, b, (((1,), (1,)), ((), ())), preferred_element_type=F32)


def tm(a, b):
    return lax.dot_general(a, b, (((0,), (0,)), ((), ())), preferred_element_type=F32)


def loop(count, body):
    def step(i, carry):
        body(i)
        return carry
    lax.fori_loop(0, count, step, 0)


class RingSum:
    def __init__(self, size, part, pair_in, relay_in, ring_in, whole, send, recv):
        me = lax.axis_index('model')
        self.core = lax.rem(me, 2)
        self.chips = size // 2
        self.chip = me // 2
        self.right = lax.rem(me + 2, size)
        self.left = lax.rem(me + size - 2, size)
        self.partner = me + 1 - 2 * self.core
        self.part, self.pair_in, self.relay_in, self.ring_in, self.whole = part, pair_in, relay_in, ring_in, whole
        self.send, self.recv = send, recv

    def base(self, core, step):
        return core * HALF + lax.rem(self.chip + step, self.chips) * PIECE

    def copy(self, n, s):
        slot = lax.rem(s, SLOTS)
        part, whole = self.part.at[slot], self.whole.at[slot]
        base = functools.partial(self.base, self.core)
        last = self.chips - 1
        if n == 0:
            src, dst, to = part.at[pl.ds((1 - self.core) * HALF, HALF)], self.pair_in.at[slot], self.partner
        elif n == 1:
            src, dst, to = part.at[pl.ds(base(2), 1)], self.relay_in.at[slot, pl.ds(0, 1)], self.right
        elif n == 2:
            src, dst, to = part.at[pl.ds(base(2) + 1, 1)], self.relay_in.at[slot, pl.ds(1, 1)], self.left
        elif n == 3:
            src, dst, to = part.at[pl.ds(base(1), PIECE)], self.ring_in.at[slot, 0], self.right
        elif n == 4:
            src, dst, to = part.at[pl.ds(base(last), PIECE)], self.ring_in.at[slot, 1], self.left
        else:
            start, length, to = {
                5: (base(0), PIECE, self.right),
                6: (base(0), PIECE, self.left),
                7: (base(0), PIECE, self.partner),
                8: (base(last), 1, self.right),
                9: (base(1) + 1, 1, self.left),
                10: (base(last), PIECE, self.partner),
                11: (base(1), PIECE, self.partner),
                12: (base(2), PIECE, self.partner),
            }[n]
            src = dst = whole.at[pl.ds(start, length)]
        return pltpu.make_async_remote_copy(
            src_ref=src, dst_ref=dst, send_sem=self.send.at[slot, n], recv_sem=self.recv.at[slot, n],
            device_id={'model': to}, device_id_type=MESH)

    def add(self, slot, block, others):
        total = self.part[slot, block].astype(F32)
        for ref in others:
            total = total + ref.astype(F32)
        return total.astype(BF16)

    def stage(self, j, s):
        slot = lax.rem(s, SLOTS)
        last = self.chips - 1
        if j == 0:
            self.copy(0, s).start()
        elif j == 1:
            self.copy(0, s).wait_recv()

            def pair(i):
                block = self.core * HALF + i
                self.part[slot, block] = self.add(slot, block, [self.pair_in[slot, i]])
            loop(HALF, pair)
            self.copy(1, s).start()
            self.copy(2, s).start()
        elif j == 2:
            self.copy(1, s).wait_recv()
            self.copy(2, s).wait_recv()
            first, second = self.base(self.core, 1), self.base(self.core, last) + 1
            self.part[slot, first] = self.add(slot, first, [self.relay_in[slot, 0]])
            self.part[slot, second] = self.add(slot, second, [self.relay_in[slot, 1]])
            self.copy(3, s).start()
            self.copy(4, s).start()
        elif j == 3:
            self.copy(3, s).wait_recv()
            self.copy(4, s).wait_recv()
            for i in range(PIECE):
                block = self.base(self.core, 0) + i
                self.whole[slot, block] = self.add(slot, block, [self.ring_in[slot, 0, i], self.ring_in[slot, 1, i]])
            for n in (5, 6, 7):
                self.copy(n, s).start()
        elif j == 4:
            self.copy(5, s).wait_recv()
            self.copy(6, s).wait_recv()
            for n in (8, 9, 10, 11):
                self.copy(n, s).start()
        elif j == 5:
            self.copy(8, s).wait_recv()
            self.copy(9, s).wait_recv()
            self.copy(12, s).start()
        else:
            for n in (7, 10, 11, 12):
                self.copy(n, s).wait_recv()
            for n in range(COPIES):
                self.copy(n, s).wait_send()


LAST = 6


def enter(size):
    me = lax.axis_index('model')
    barrier = pltpu.get_barrier_semaphore()
    for other in (lax.rem(me + 2, size), lax.rem(me + size - 2, size), me + 1 - 2 * lax.rem(me, 2)):
        pl.semaphore_signal(barrier, inc=1, device_id={'model': other}, device_id_type=MESH)
    pl.semaphore_wait(barrier, 3)


def drain_count(points, start):
    return (start + LAST) // points


def make_progress(count, points, sums):
    def progress(t, i):
        for ring, start, consume in sums:
            for j in range(LAST, 0, -1):
                if (start + j - i) % points:
                    continue
                s = t - (start + j - i) // points

                @pl.when(jnp.logical_and(s >= 0, s < count))
                def _(ring=ring, consume=consume, j=j, s=s):
                    ring.stage(j, s)
                    if j == LAST:
                        consume(s)
    return progress


def norm_stats(x):
    mean = jnp.mean(x, axis=-1, keepdims=True)
    centered = x - mean
    var = jnp.mean(centered * centered, axis=-1, keepdims=True)
    inv = lax.rsqrt(var + NORM_EPS)
    return centered * inv, inv


def norm_back(x, gain, d_normed):
    unit, inv = norm_stats(x)
    d_unit = d_normed * gain
    mean_d = jnp.mean(d_unit, axis=-1, keepdims=True)
    mean_du = jnp.mean(d_unit * unit, axis=-1, keepdims=True)
    return inv * (d_unit - mean_d - unit * mean_du), d_normed * unit


def probs_of(q, k, seg_col, seg_row, row0, scale):
    scores = mt(q, k) * scale
    q_pos = row0 + lax.broadcasted_iota(jnp.int32, scores.shape, 0)
    k_pos = lax.broadcasted_iota(jnp.int32, scores.shape, 1)
    allowed = jnp.logical_and(seg_col == seg_row, q_pos >= k_pos)
    scores = jnp.where(allowed, scores, -1e30)
    e = jnp.exp(scores - jnp.max(scores, axis=-1, keepdims=True))
    return e * (1.0 / jnp.sum(e, axis=-1, keepdims=True))


def head_masks(width, head_dim):
    lane = lax.broadcasted_iota(jnp.int32, (1, width), 1)
    return [jnp.logical_and(lane >= h * head_dim, lane < (h + 1) * head_dim) for h in range(width // head_dim)]


Q_ROWS = 128


def attn_forward_kernel(size, head_dim, tok_hbm, seg_row, seg_col, gain, w_qkv, w_out,
                        x1_hbm, a_hbm, saved_hbm,
                        x, a, saved, part, pair_in, relay_in, ring_in, whole,
                        in_sem, x1_sem, a_sem, saved_sem, send, recv):
    count = x.shape[0]
    rows, hidden = x.shape[1] * x.shape[2], x.shape[3]
    width = w_out.shape[0]
    scale = head_dim ** -0.5
    points, start = 3, 2
    steps = count + drain_count(points, start)

    def x_in(s):
        return pltpu.make_async_copy(tok_hbm.at[s], x.at[s], in_sem.at[s])

    def x_out(s):
        return pltpu.make_async_copy(x.at[s], x1_hbm.at[s], x1_sem.at[s])

    def a_out(s):
        slot = lax.rem(s, 2)
        return pltpu.make_async_copy(a.at[slot], a_hbm.at[s], a_sem.at[slot])

    def saved_out(s):
        slot = lax.rem(s, 2)
        return pltpu.make_async_copy(saved.at[slot], saved_hbm.at[s], saved_sem.at[slot])

    loop(count, lambda s: x_in(s).start())
    enter(size)
    ring = RingSum(size, part, pair_in, relay_in, ring_in, whole, send, recv)

    def consume(s):
        slot = lax.rem(s, SLOTS)

        def block(r):
            x[s, r] = (x[s, r].astype(F32) + whole[slot, r].astype(F32)).astype(BF16)
        loop(BLOCKS, block)
        x_out(s).start()

    progress = make_progress(count, points, [(ring, start, consume)])
    masks = head_masks(width, head_dim)

    def step(t):
        slot2 = lax.rem(t, 2)

        @pl.when(t < count)
        def _():
            x_in(t).wait()

            @pl.when(t >= 2)
            def _():
                a_out(t - 2).wait()
                saved_out(t - 2).wait()

            def block(r):
                unit, _ = norm_stats(x[t, r].astype(F32))
                a[slot2, r] = (unit * gain[...]).astype(BF16)
            loop(BLOCKS, block)
            a_out(t).start()

        progress(t, 0)

        @pl.when(t < count)
        def _():
            a_rows = a[slot2].reshape(rows, hidden)
            saved[slot2, :, :3 * width] = mm(a_rows, w_qkv[...]).astype(BF16)

            def q_block(i):
                row0 = pl.multiple_of(i * Q_ROWS, Q_ROWS)
                part_rows = pl.ds(row0, Q_ROWS)
                q = saved[slot2, part_rows, 0:width]
                k = saved[slot2, :, width:2 * width]
                v = saved[slot2, :, 2 * width:3 * width]
                out = None
                for mask in masks:
                    probs = probs_of(jnp.where(mask, q, 0).astype(BF16), k, seg_col[t, part_rows], seg_row[t], row0, scale)
                    head = mm(probs.astype(BF16), v)
                    out = head if out is None else jnp.where(mask, head, out)
                saved[slot2, part_rows, 3 * width:4 * width] = out.astype(BF16)
            loop(rows // Q_ROWS, q_block)

        progress(t, 1)

        @pl.when(t < count)
        def _():
            slot = lax.rem(t, SLOTS)
            half = rows // 2
            for h in range(2):
                proj = mm(saved[slot2, h * half:(h + 1) * half, 3 * width:4 * width], w_out[...])
                part[slot, h * HALF:(h + 1) * HALF] = proj.astype(BF16).reshape(HALF, rows // BLOCKS, hidden)
            saved_out(t).start()
            ring.stage(0, t)

        progress(t, 2)

    loop(steps, step)
    loop(count, lambda s: x_out(s).wait())
    for s in (count - 2, count - 1):
        a_out(s).wait()
        saved_out(s).wait()


def mlp_kernel(size, x1_hbm, dout_hbm, gain, w_up, w_down,
               out_hbm, db_hbm, dw_up_out, dw_down_out,
               x, d, b, pre, d_hid, u, d_pre, dw_up, dw_down,
               part1, pair_in1, relay_in1, ring_in1, whole1,
               part2, pair_in2, relay_in2, ring_in2, whole2,
               x_sem, d_sem, out_sem, db_sem, send1, recv1, send2, recv2):
    count = x.shape[0]
    block_rows, hidden = x.shape[2], x.shape[3]
    rows = BLOCKS * block_rows
    points, start = 4, 2
    steps = count + drain_count(points, start)

    def x_in(s):
        return pltpu.make_async_copy(x1_hbm.at[s], x.at[s], x_sem.at[s])

    def x_out(s):
        return pltpu.make_async_copy(x.at[s], out_hbm.at[s], out_sem.at[s])

    def d_in(s):
        slot = lax.rem(s, 2)
        return pltpu.make_async_copy(dout_hbm.at[s], d.at[slot], d_sem.at[slot])

    def db_out(s):
        slot = lax.rem(s, SLOTS)
        return pltpu.make_async_copy(whole1.at[slot], db_hbm.at[s], db_sem.at[slot])

    d_in(0).start()
    loop(count, lambda s: x_in(s).start())
    enter(size)
    ring1 = RingSum(size, part1, pair_in1, relay_in1, ring_in1, whole1, send1, recv1)
    ring2 = RingSum(size, part2, pair_in2, relay_in2, ring_in2, whole2, send2, recv2)
    dw_up[...] = jnp.zeros_like(dw_up)
    dw_down[...] = jnp.zeros_like(dw_down)

    def consume1(s):
        db_out(s).start()

    def consume2(s):
        slot = lax.rem(s, SLOTS)

        def block(r):
            x[s, r] = (x[s, r].astype(F32) + whole2[slot, r].astype(F32)).astype(BF16)
        loop(BLOCKS, block)
        x_out(s).start()

    progress = make_progress(count, points, [(ring1, start, consume1), (ring2, start, consume2)])

    def step(t):
        slot = lax.rem(t, SLOTS)
        slot2 = lax.rem(t, 2)

        @pl.when(t < count)
        def _():
            x_in(t).wait()
            d_in(t).wait()

            @pl.when(t + 1 < count)
            def _():
                d_in(t + 1).start()

            def block(r):
                unit, _ = norm_stats(x[t, r].astype(F32))
                b[r] = (unit * gain[...]).astype(BF16)
            loop(BLOCKS, block)
            pre[...] = mm(b[...].reshape(rows, hidden), w_up[...])

        progress(t, 0)

        @pl.when(t < count)
        def _():
            d_hid[...] = mt(d[slot2].reshape(rows, hidden), w_down[...])

            def block(r):
                part_rows = pl.ds(pl.multiple_of(r * block_rows, block_rows), block_rows)
                v = pre[part_rows]
                v2 = v * v
                c = 0.7978845608028654
                th = jnp.tanh(c * (v + 0.044715 * (v * v2)))
                u[part_rows] = (0.5 * v * (1.0 + th)).astype(BF16)
                slope = 0.5 * (1.0 + th) + 0.5 * v * (1.0 - th * th) * (c * (1.0 + 3.0 * 0.044715 * v2))
                d_pre[part_rows] = (d_hid[part_rows].astype(BF16).astype(F32) * slope).astype(BF16)
            loop(BLOCKS, block)

        progress(t, 1)

        @pl.when(t < count)
        def _():
            @pl.when(t >= SLOTS)
            def _():
                db_out(t - SLOTS).wait()
            half = rows // 2
            for h in range(2):
                d_b = mt(d_pre[h * half:(h + 1) * half], w_up[...])
                part1[slot, h * HALF:(h + 1) * HALF] = d_b.astype(BF16).reshape(HALF, block_rows, hidden)
            ring1.stage(0, t)
            for h in range(2):
                down = mm(u[h * half:(h + 1) * half], w_down[...])
                part2[slot, h * HALF:(h + 1) * HALF] = down.astype(BF16).reshape(HALF, block_rows, hidden)
            ring2.stage(0, t)

        progress(t, 2)

        @pl.when(t < count)
        def _():
            dw_up[...] += tm(b[...].reshape(rows, hidden), d_pre[...])
            dw_down[...] += tm(u[...], d[slot2].reshape(rows, hidden))

        progress(t, 3)

    loop(steps, step)
    dw_up_out[...] = dw_up[...].astype(BF16)
    dw_down_out[...] = dw_down[...].astype(BF16)
    loop(count, lambda s: x_out(s).wait())
    for s in range(count - SLOTS, count):
        db_out(s).wait()


def attn_backward_kernel(size, head_dim, tok_hbm, dout_hbm, x1_hbm, db_hbm, a_hbm, saved_hbm,
                         seg_row, seg_col, gain_attn, gain_mlp, w_qkv, w_out,
                         dtok_hbm, dw_qkv_out, dw_out_out, dg_attn_out, dg_mlp_out,
                         x, d, x1, db, a, saved, d_heads, probs, d_scores, d_qkv,
                         dw_qkv, dw_out, dg_attn, dg_mlp,
                         part, pair_in, relay_in, ring_in, whole,
                         x_sem, d_sem, x1_sem, db_sem, a_sem, saved_sem, out_sem, send, recv):
    count = x.shape[0]
    block_rows, hidden = x.shape[2], x.shape[3]
    rows = BLOCKS * block_rows
    width = w_out.shape[0]
    scale = head_dim ** -0.5
    points, start = 3, 2
    steps = count + drain_count(points, start)

    def whole_in(s):
        return [pltpu.make_async_copy(tok_hbm.at[s], x.at[s], x_sem.at[s]),
                pltpu.make_async_copy(dout_hbm.at[s], d.at[s], d_sem.at[s])]

    def slot_in(s):
        slot = lax.rem(s, 2)
        return [pltpu.make_async_copy(x1_hbm.at[s], x1.at[slot], x1_sem.at[slot]),
                pltpu.make_async_copy(db_hbm.at[s], db.at[slot], db_sem.at[slot]),
                pltpu.make_async_copy(a_hbm.at[s], a.at[slot], a_sem.at[slot]),
                pltpu.make_async_copy(saved_hbm.at[s], saved.at[slot], saved_sem.at[slot])]

    def x_out(s):
        return pltpu.make_async_copy(x.at[s], dtok_hbm.at[s], out_sem.at[s])

    for c in slot_in(0) + whole_in(0):
        c.start()
    enter(size)
    ring = RingSum(size, part, pair_in, relay_in, ring_in, whole, send, recv)
    for ref in (dw_qkv, dw_out, dg_attn, dg_mlp):
        ref[...] = jnp.zeros_like(ref)

    def rows_sum(v):
        return jnp.sum(v.reshape(v.shape[0] // 8, 8, hidden), axis=0)

    def consume(s):
        slot = lax.rem(s, SLOTS)

        def block(r):
            dx, dg = norm_back(x[s, r].astype(F32), gain_attn[...], whole[slot, r].astype(F32))
            dg_attn[...] += rows_sum(dg)
            x[s, r] = (d[s, r].astype(F32) + dx).astype(BF16)
        loop(BLOCKS, block)
        x_out(s).start()

    progress = make_progress(count, points, [(ring, start, consume)])
    masks = head_masks(width, head_dim)

    def step(t):
        slot = lax.rem(t, SLOTS)
        slot2 = lax.rem(t, 2)

        @pl.when(t < count)
        def _():
            for c in slot_in(t) + whole_in(t):
                c.wait()

            @pl.when(t + 1 < count)
            def _():
                for c in slot_in(t + 1) + whole_in(t + 1):
                    c.start()

            def block(r):
                dx, dg = norm_back(x1[slot2, r].astype(F32), gain_mlp[...], db[slot2, r].astype(F32))
                dg_mlp[...] += rows_sum(dg)
                d[t, r] = (d[t, r].astype(F32) + dx).astype(BF16)
            loop(BLOCKS, block)
            d_rows = d[t].reshape(rows, hidden)
            d_heads[...] = mt(d_rows, w_out[...]).astype(BF16)

        progress(t, 0)

        @pl.when(t < count)
        def _():
            q_all = saved[slot2, :, 0:width]
            k_all = saved[slot2, :, width:2 * width]
            v_all = saved[slot2, :, 2 * width:3 * width]
            for h, mask in enumerate(masks):
                def q_block(i):
                    row0 = pl.multiple_of(i * Q_ROWS, Q_ROWS)
                    part_rows = pl.ds(row0, Q_ROWS)
                    q = jnp.where(mask, saved[slot2, part_rows, 0:width], 0).astype(BF16)
                    d_head = jnp.where(mask, d_heads[part_rows], 0).astype(BF16)
                    p = probs_of(q, saved[slot2, :, width:2 * width], seg_col[t, part_rows], seg_row[t], row0, scale)
                    d_p = mt(d_head, saved[slot2, :, 2 * width:3 * width])
                    row_dot = jnp.sum(d_p * p, axis=-1, keepdims=True)
                    probs[part_rows] = p.astype(BF16)
                    d_scores[part_rows] = (p * (d_p - row_dot) * scale).astype(BF16)
                loop(rows // Q_ROWS, q_block)
                d_q = mm(d_scores[...], k_all).astype(BF16)
                d_k = tm(d_scores[...], q_all).astype(BF16)
                d_v = tm(probs[...], d_heads[...]).astype(BF16)
                for j, value in enumerate((d_q, d_k, d_v)):
                    cols = slice(j * width, (j + 1) * width)
                    d_qkv[:, cols] = value if h == 0 else jnp.where(mask, value, d_qkv[:, cols])

        progress(t, 1)

        @pl.when(t < count)
        def _():
            half = rows // 2
            for h in range(2):
                d_a = mt(d_qkv[h * half:(h + 1) * half], w_qkv[...])
                part[slot, h * HALF:(h + 1) * HALF] = d_a.astype(BF16).reshape(HALF, block_rows, hidden)
            ring.stage(0, t)
            dw_qkv[...] += tm(a[slot2].reshape(rows, hidden), d_qkv[...])
            dw_out[...] += tm(saved[slot2, :, 3 * width:4 * width], d[t].reshape(rows, hidden))

        progress(t, 2)

    loop(steps, step)
    dw_qkv_out[...] = dw_qkv[...].astype(BF16)
    dw_out_out[...] = dw_out[...].astype(BF16)
    dg_attn_out[...] = jnp.sum(dg_attn[...], axis=0, keepdims=True)
    dg_mlp_out[...] = jnp.sum(dg_mlp[...], axis=0, keepdims=True)
    loop(count, lambda s: x_out(s).wait())


def ring_buffers(block_rows, hidden):
    return [
        pltpu.VMEM((SLOTS, BLOCKS, block_rows, hidden), BF16),
        pltpu.VMEM((SLOTS, HALF, block_rows, hidden), BF16),
        pltpu.VMEM((SLOTS, 2, block_rows, hidden), BF16),
        pltpu.VMEM((SLOTS, 2, PIECE, block_rows, hidden), BF16),
        pltpu.VMEM((SLOTS, BLOCKS, block_rows, hidden), BF16),
    ]


def ring_sems():
    return [pltpu.SemaphoreType.DMA((SLOTS, COPIES)), pltpu.SemaphoreType.DMA((SLOTS, COPIES))]


def run_kernel(kernel, ident, outs, out_vmem, args, in_vmem, scratch):
    def spec(in_vmem):
        return pl.BlockSpec(memory_space=pltpu.VMEM if in_vmem else pl.ANY)
    return pl.pallas_call(
        kernel,
        out_shape=[jax.ShapeDtypeStruct(s, t) for s, t in outs],
        in_specs=[spec(v) for v in in_vmem],
        out_specs=[spec(v) for v in out_vmem],
        scratch_shapes=scratch,
        compiler_params=pltpu.CompilerParams(collective_id=ident, has_side_effects=True, vmem_limit_bytes=VMEM_LIMIT),
        name=f'layer_part_{ident}',
    )(*args)


def solution(mesh):
    size = mesh.shape['model']
    dma = pltpu.SemaphoreType.DMA

    def device_step(tokens, seg_ids, d_out, gain_attn, gain_mlp, w_qkv, w_out, w_up, w_down):
        count, seq_len, hidden = tokens.shape
        heads, head_dim = w_qkv.shape[1], w_qkv.shape[3]
        width = heads * head_dim
        inner = w_up.shape[1]
        block_rows = seq_len // BLOCKS
        act = (count, BLOCKS, block_rows, hidden)
        one = (BLOCKS, block_rows, hidden)
        x = tokens.reshape(act)
        d = d_out.reshape(act)
        seg_row = seg_ids.reshape(count, 1, seq_len)
        seg_col = seg_ids.reshape(count, seq_len, 1)
        g_attn = gain_attn.astype(F32).reshape(1, hidden)
        g_mlp = gain_mlp.astype(F32).reshape(1, hidden)
        wqkv = w_qkv.transpose(0, 2, 1, 3).reshape(hidden, 3 * width)
        wout = w_out.reshape(width, hidden)

        x1, a, saved = run_kernel(
            functools.partial(attn_forward_kernel, size, head_dim), 1,
            [(act, BF16), (act, BF16), ((count, seq_len, 4 * width), BF16)], [False] * 3,
            [x, seg_row, seg_col, g_attn, wqkv, wout], [False] + [True] * 5,
            [pltpu.VMEM(act, BF16), pltpu.VMEM((2,) + one, BF16), pltpu.VMEM((2, seq_len, 4 * width), BF16)]
            + ring_buffers(block_rows, hidden)
            + [dma((count,)), dma((count,)), dma((2,)), dma((2,))] + ring_sems())

        layer_out, d_b, d_w_up, d_w_down = run_kernel(
            functools.partial(mlp_kernel, size), 2,
            [(act, BF16), (act, BF16), ((hidden, inner), BF16), ((inner, hidden), BF16)], [False, False, True, True],
            [x1, d, g_mlp, w_up, w_down], [False, False, True, True, True],
            [pltpu.VMEM(act, BF16), pltpu.VMEM((2,) + one, BF16), pltpu.VMEM(one, BF16),
             pltpu.VMEM((seq_len, inner), F32), pltpu.VMEM((seq_len, inner), F32),
             pltpu.VMEM((seq_len, inner), BF16), pltpu.VMEM((seq_len, inner), BF16),
             pltpu.VMEM((hidden, inner), F32), pltpu.VMEM((inner, hidden), F32)]
            + ring_buffers(block_rows, hidden) + ring_buffers(block_rows, hidden)
            + [dma((count,)), dma((2,)), dma((count,)), dma((SLOTS,))] + ring_sems() + ring_sems())

        d_tokens, dw_qkv, dw_out, dg_attn, dg_mlp = run_kernel(
            functools.partial(attn_backward_kernel, size, head_dim), 3,
            [(act, BF16), ((hidden, 3 * width), BF16), ((width, hidden), BF16), ((1, hidden), F32), ((1, hidden), F32)],
            [False] + [True] * 4,
            [x, d, x1, d_b, a, saved, seg_row, seg_col, g_attn, g_mlp, wqkv, wout], [False] * 6 + [True] * 6,
            [pltpu.VMEM(act, BF16), pltpu.VMEM(act, BF16)] + [pltpu.VMEM((2,) + one, BF16)] * 3
            + [pltpu.VMEM((2, seq_len, 4 * width), BF16), pltpu.VMEM((seq_len, width), BF16),
               pltpu.VMEM((seq_len, seq_len), BF16), pltpu.VMEM((seq_len, seq_len), BF16),
               pltpu.VMEM((seq_len, 3 * width), BF16),
               pltpu.VMEM((hidden, 3 * width), F32), pltpu.VMEM((width, hidden), F32),
               pltpu.VMEM((8, hidden), F32), pltpu.VMEM((8, hidden), F32)]
            + ring_buffers(block_rows, hidden)
            + [dma((count,)), dma((count,))] + [dma((2,))] * 4 + [dma((count,))] + ring_sems())

        d_w_qkv = dw_qkv.reshape(hidden, 3, heads, head_dim).transpose(0, 2, 1, 3)
        return (layer_out.reshape(tokens.shape), d_tokens.reshape(tokens.shape), d_w_qkv,
                dw_out.reshape(w_out.shape), d_w_up, d_w_down, dg_attn.reshape(hidden), dg_mlp.reshape(hidden))

    in_specs = (P('data', None, None), P('data', None), P('data', None, None), P(), P(), P(None, 'model', None, None), P('model', None, None), P(None, 'model'), P('model', None))
    out_specs = (P('data', None, None), P('data', None, None), P('data', 'model', None, None), P(('data', 'model'), None, None), P('data', 'model'), P(('data', 'model'), None), P('data'), P('data'))
    return jax.shard_map(device_step, mesh=mesh, in_specs=in_specs, out_specs=out_specs, check_vma=False)
```

time: 809 us -> 537 us (0.66)
  Pallas kernels: 0 us -> 505 us
  waiting for transfers between devices: 460 us -> 0 us
  matrix products: 202 us -> 0 us
  other arithmetic: 113 us -> 2.55 us
  local copies, waits for them, and re-layouts: 11.6 us -> 28.2 us
  between operations: 14.9 us -> 0.69 us
    pallas_call x0 -> x3, Pallas kernels: none -> 505 us  [run_kernel(): pl.pallas_call(kernel, out_shape=[jax.ShapeDtypeStruct(s, t) for s, t in...]
    psum x5 -> x0, waiting for transfers between devices: 460 us -> none  [the longest x2 198 us: forward_pass(): reduce_sum(jnp.einsum('bnsd,ndh->bsh', attn_heads, w_out, preferred_eleme...]
    dot_general x19 -> x0, matrix products: 179 us -> none  [the longest x1 23.6 us: backward_pass(): jnp.einsum('bnqk,bnqd->bnkd', d_scores, qkv_all[0], preferred_element_typ...]
    reduce_sum x12 -> x0, other arithmetic: 81.6 us -> none  [the longest x4 43.3 us: layer_norm(): return centered * lax.rsqrt(var_val + NORM_EPS) * gain_vec]
    convert_element_type x5 -> x0, other arithmetic: 29.1 us -> none  [the longest x1 10.6 us: forward_pass(): layer_out = (resid_f32 + mlp_down.astype(jnp.float32)).astype(jnp.bfloat16)]
    sub x2 -> x0, matrix products: 22.5 us -> none  [forward_pass(): attn_probs = jax.nn.softmax(jnp.where(allowed, scores, -1e+30), axis=-1)]
    unnamed x81 -> x19, local copies, waits for them, and re-layouts: 11.6 us -> 21.6 us
  transfers between devices with their start and end apart: 5 -> 0, of which waited for: 5 -> 0; matrix products, arithmetic and copies ran while one was open for 4% -> 0% of each run, Pallas kernels for 0% -> 0%
where the time goes in v1:
time: 537 us
  Pallas kernels  505 us (94%)
  local copies, waits for them, and re-layouts  28.2 us (5%)
    pallas_call x3, Pallas kernels, run_kernel(): pl.pallas_call(kernel, out_shape=[jax.ShapeDtypeStruct(s, t) for s, t in...  505 us
    unnamed x19, local copies, waits for them, and re-layouts  21.6 us

profile of v1, /device:TPU:81, one launch (start us, length us, event | category | flops | bytes accessed | tf_op | source)
XLA Modules:
  0.0 536.7 jit_solution(17235901748874968930)
XLA Ops:
  0.6 1.3 reshape.78
  1.9 1.3 reshape.80
  3.2 1.3 reshape.63.seg_row
  4.5 1.2 copy.19
  5.7 1.2 copy.21.w_qkv
  6.9 2.7 copy.20.seg_col
  9.5 150.1 %layer_part_1.1 = (bf16[8,16,32,1024]{3,2,1,0:T(8,128)(2,1)}, bf16[8,16,32,1024]{3,2,1,0:T(8,128)(2,1)}, bf16[8,512,512]{2,1,0:T(8,128)(2,1)}) custom-call(bf16[8,16,32,1024]{3,2,1,0:T(8,128)(2,1)} %bitcast.19, s32[8,1,512]{2,1,0:T(1,128)} %reshape.63.seg_row, s32[8,512,1]{2,1,0:T(8,128)} %copy.20.seg_col, f32[1,1024]{1,0:T(1,128)} %bitcast.29, ...), custom_call_target="tpu_custom_call" | custom-call | tf_op jit(solution)/shard_map/layer_part_1/pallas_call | solution.py:559
  159.7 189.5 %layer_part_2.1 = (bf16[8,16,32,1024]{3,2,1,0:T(8,128)(2,1)}, bf16[8,16,32,1024]{3,2,1,0:T(8,128)(2,1)}, bf16[1024,512]{1,0:T(8,128)(2,1)}, bf16[512,1024]{1,0:T(8,128)(2,1)}) custom-call(bf16[8,16,32,1024]{3,2,1,0:T(8,128)(2,1)} %get-tuple-element.20.x1_hbm, bf16[8,16,32,1024]{3,2,1,0:T(8,128)(2,1)} %bitcast.17, f32[1,1024]{1,0:T(1,128)} %bitcast.31, ...), custom_call_target="tpu_custom_call" | custom-call | tf_op jit(solution)/shard_map/layer_part_2/pallas_call | solution.py:559
  349.1 165.7 %layer_part_3.1 = (bf16[8,16,32,1024]{3,2,1,0:T(8,128)(2,1)}, bf16[1024,384]{1,0:T(8,128)(2,1)}, bf16[128,1024]{1,0:T(8,128)(2,1)}, f32[1,1024]{1,0:T(1,128)}, f32[1,1024]{1,0:T(1,128)}) custom-call(bf16[8,16,32,1024]{3,2,1,0:T(8,128)(2,1)} %bitcast.20, bf16[8,16,32,1024]{3,2,1,0:T(8,128)(2,1)} %bitcast.18, ...), custom_call_target="tpu_custom_call" | custom-call | tf_op jit(solution)/shard_map/layer_part_3/pallas_call | solution.py:559
  514.9 1.4 copy.24
  516.3 0.9 copy.25
  517.2 7.8 %copy.33 = bf16[8,512,1024]{2,1,0:T(8,128)(2,1)} copy(bf16[8,512,1024]{2,1,0:T(8,128)(2,1)} %bitcast.21) | data formatting | bytes 16777216
  525.0 0.0 copy-start.2
  525.0 0.0 copy-start.1
  525.0 0.0 copy-start
  525.0 0.0 copy-start.4
  525.0 0.0 copy-start.3
  525.0 7.9 %copy.34 = bf16[8,512,1024]{2,1,0:T(8,128)(2,1)} copy(bf16[8,512,1024]{2,1,0:T(8,128)(2,1)} %bitcast.22) | data formatting | bytes 16777216
  532.9 0.0 copy-done.2
  532.9 0.7 copy.35
  533.6 0.0 copy-done.1
  533.6 1.0 copy.36
  534.6 0.0 copy-done
  534.6 1.0 copy.37
  535.6 0.0 copy-done.4
  535.6 0.6 copy.38
  536.1 0.0 copy-done.3
  536.1 0.6 copy.39
Async XLA Ops:
  525.0 7.9 %copy-start.2 = (bf16[128,1024]{1,0:T(8,128)(2,1)S(1)}, bf16[128,1024]{1,0:T(8,128)(2,1)}, u32[]{:S(2)}) copy-start(bf16[128,1024]{1,0:T(8,128)(2,1)} %get-tuple-element.27) | copy-start | bytes 786436
  525.0 8.6 %copy-start.1 = (bf16[1024,512]{1,0:T(8,128)(2,1)S(1)}, bf16[1024,512]{1,0:T(8,128)(2,1)}, u32[]{:S(2)}) copy-start(bf16[1024,512]{1,0:T(8,128)(2,1)} %get-tuple-element.52) | copy-start | bytes 3145732
  525.0 9.6 %copy-start = (bf16[512,1024]{1,0:T(8,128)(2,1)S(1)}, bf16[512,1024]{1,0:T(8,128)(2,1)}, u32[]{:S(2)}) copy-start(bf16[512,1024]{1,0:T(8,128)(2,1)} %get-tuple-element.53) | copy-start | bytes 3145732
  525.0 10.6 %copy-start.4 = (f32[1,1024]{1,0:T(1,128)S(1)}, f32[1,1024]{1,0:T(1,128)}, u32[]{:S(2)}) copy-start(f32[1,1024]{1,0:T(1,128)} %get-tuple-element.30) | copy-start | bytes 12292
  525.0 11.2 %copy-start.3 = (f32[1,1024]{1,0:T(1,128)S(1)}, f32[1,1024]{1,0:T(1,128)}, u32[]{:S(2)}) copy-start(f32[1,1024]{1,0:T(1,128)} %get-tuple-element.31) | copy-start | bytes 12292

commit v2 on v0

v2 whole, which is shorter than its diff:
```python
import functools
import jax
import jax.numpy as jnp
from jax import lax
from jax.experimental import pallas as pl
from jax.experimental.pallas import tpu as pltpu
from jax.sharding import PartitionSpec as P

NORM_EPS = 1e-5
MESH = pl.DeviceIdType.MESH
F32 = jnp.float32
BF16 = jnp.bfloat16
SLOTS = 2
SPACING = 2
POINTS = 12
BLOCKS = 16
HALF = BLOCKS // 2
PIECE = 2
COPIES = 13
VMEM_LIMIT = 66 * 1000 * 1000


def mm(a, b):
    return lax.dot_general(a, b, (((1,), (0,)), ((), ())), preferred_element_type=F32)


def mt(a, b):
    return lax.dot_general(a, b, (((1,), (1,)), ((), ())), preferred_element_type=F32)


def tm(a, b):
    return lax.dot_general(a, b, (((0,), (0,)), ((), ())), preferred_element_type=F32)


def loop(count, body):
    def step(i, carry):
        body(i)
        return carry
    lax.fori_loop(0, count, step, 0)


class RingSum:
    def __init__(self, size, part, pair_in, relay_in, ring_in, whole, send, recv):
        me = lax.axis_index('model')
        self.core = lax.rem(me, 2)
        self.chips = size // 2
        self.chip = me // 2
        self.right = lax.rem(me + 2, size)
        self.left = lax.rem(me + size - 2, size)
        self.partner = me + 1 - 2 * self.core
        self.part, self.pair_in, self.relay_in, self.ring_in, self.whole = part, pair_in, relay_in, ring_in, whole
        self.send, self.recv = send, recv

    def base(self, core, step):
        return core * HALF + lax.rem(self.chip + step, self.chips) * PIECE

    def copy(self, n, s):
        slot = lax.rem(s, SLOTS)
        part, whole = self.part.at[slot], self.whole.at[slot]
        base = functools.partial(self.base, self.core)
        last = self.chips - 1
        if n == 0:
            src, dst, to = part.at[pl.ds((1 - self.core) * HALF, HALF)], self.pair_in.at[slot], self.partner
        elif n == 1:
            src, dst, to = part.at[pl.ds(base(2), 1)], self.relay_in.at[slot, pl.ds(0, 1)], self.right
        elif n == 2:
            src, dst, to = part.at[pl.ds(base(2) + 1, 1)], self.relay_in.at[slot, pl.ds(1, 1)], self.left
        elif n == 3:
            src, dst, to = part.at[pl.ds(base(1), PIECE)], self.ring_in.at[slot, 0], self.right
        elif n == 4:
            src, dst, to = part.at[pl.ds(base(last), PIECE)], self.ring_in.at[slot, 1], self.left
        else:
            start, length, to = {
                5: (base(0), PIECE, self.right),
                6: (base(0), PIECE, self.left),
                7: (base(0), PIECE, self.partner),
                8: (base(last), 1, self.right),
                9: (base(1) + 1, 1, self.left),
                10: (base(last), PIECE, self.partner),
                11: (base(1), PIECE, self.partner),
                12: (base(2), PIECE, self.partner),
            }[n]
            src = dst = whole.at[pl.ds(start, length)]
        return pltpu.make_async_remote_copy(
            src_ref=src, dst_ref=dst, send_sem=self.send.at[slot, n], recv_sem=self.recv.at[slot, n],
            device_id={'model': to}, device_id_type=MESH)

    def add(self, slot, block, others):
        total = self.part[slot, block].astype(F32)
        for ref in others:
            total = total + ref.astype(F32)
        return total.astype(BF16)

    def stage(self, j, s):
        slot = lax.rem(s, SLOTS)
        last = self.chips - 1
        if j == 0:
            self.copy(0, s).start()
        elif j == 1:
            self.copy(0, s).wait_recv()

            def pair(i):
                block = self.core * HALF + i
                self.part[slot, block] = self.add(slot, block, [self.pair_in[slot, i]])
            loop(HALF, pair)
            self.copy(1, s).start()
            self.copy(2, s).start()
        elif j == 2:
            self.copy(1, s).wait_recv()
            self.copy(2, s).wait_recv()
            first, second = self.base(self.core, 1), self.base(self.core, last) + 1
            self.part[slot, first] = self.add(slot, first, [self.relay_in[slot, 0]])
            self.part[slot, second] = self.add(slot, second, [self.relay_in[slot, 1]])
            self.copy(3, s).start()
            self.copy(4, s).start()
        elif j == 3:
            self.copy(3, s).wait_recv()
            self.copy(4, s).wait_recv()
            for i in range(PIECE):
                block = self.base(self.core, 0) + i
                self.whole[slot, block] = self.add(slot, block, [self.ring_in[slot, 0, i], self.ring_in[slot, 1, i]])
            for n in (5, 6, 7):
                self.copy(n, s).start()
        elif j == 4:
            self.copy(5, s).wait_recv()
            self.copy(6, s).wait_recv()
            for n in (8, 9, 10, 11):
                self.copy(n, s).start()
        elif j == 5:
            self.copy(8, s).wait_recv()
            self.copy(9, s).wait_recv()
            self.copy(12, s).start()
        else:
            for n in (7, 10, 11, 12):
                self.copy(n, s).wait_recv()
            for n in range(COPIES):
                self.copy(n, s).wait_send()


LAST = 6


def enter(size):
    me = lax.axis_index('model')
    barrier = pltpu.get_barrier_semaphore()
    for other in (lax.rem(me + 2, size), lax.rem(me + size - 2, size), me + 1 - 2 * lax.rem(me, 2)):
        pl.semaphore_signal(barrier, inc=1, device_id={'model': other}, device_id_type=MESH)
    pl.semaphore_wait(barrier, 3)


def make_progress(count, points, sums):
    def progress(t, i):
        for ring, lead, start, consume in sums:
            for j in range(LAST, 0, -1):
                ahead = start + SPACING * j - i
                if ahead % points:
                    continue
                s = t - lead - ahead // points

                @pl.when(jnp.logical_and(s >= 0, s < count))
                def _(ring=ring, consume=consume, j=j, s=s):
                    ring.stage(j, s)
                    if j == LAST and consume is not None:
                        consume(s)
    return progress


def norm_stats(x):
    mean = jnp.mean(x, axis=-1, keepdims=True)
    centered = x - mean
    var = jnp.mean(centered * centered, axis=-1, keepdims=True)
    inv = lax.rsqrt(var + NORM_EPS)
    return centered * inv, inv


def norm_back(x, gain, d_normed):
    unit, inv = norm_stats(x)
    d_unit = d_normed * gain
    mean_d = jnp.mean(d_unit, axis=-1, keepdims=True)
    mean_du = jnp.mean(d_unit * unit, axis=-1, keepdims=True)
    return inv * (d_unit - mean_d - unit * mean_du), d_normed * unit


def probs_of(q, k, seg_col, seg_row, row0, scale):
    scores = mt(q, k) * scale
    q_pos = row0 + lax.broadcasted_iota(jnp.int32, scores.shape, 0)
    k_pos = lax.broadcasted_iota(jnp.int32, scores.shape, 1)
    allowed = jnp.logical_and(seg_col == seg_row, q_pos >= k_pos)
    scores = jnp.where(allowed, scores, -1e30)
    e = jnp.exp(scores - jnp.max(scores, axis=-1, keepdims=True))
    return e * (1.0 / jnp.sum(e, axis=-1, keepdims=True))


def head_masks(width, head_dim):
    lane = lax.broadcasted_iota(jnp.int32, (1, width), 1)
    return [jnp.logical_and(lane >= h * head_dim, lane < (h + 1) * head_dim) for h in range(width // head_dim)]


Q_ROWS = 128
X_SLOTS = 5
D_SLOTS = 4
A_SLOTS = 3


def layer_kernel(size, head_dim, *refs):
    (tok_hbm, dout_hbm, seg_row, seg_col, gain_attn, gain_mlp, w_qkv, w_out, w_up, w_down,
     out_hbm, dtok_hbm, dw_qkv_out, dw_out_out, dw_up_out, dw_down_out, dg_attn_out, dg_mlp_out,
     x, d, x1, a, saved, b, pre, d_hid, u, d_pre, d_heads, probs, d_scores, d_qkv,
     dw_qkv, dw_out, dw_up, dw_down, dg_attn, dg_mlp,
     x_sem, d_sem, out_sem, dtok_sem) = refs[:42]
    rings = [RingSum(size, *refs[42 + 7 * n:49 + 7 * n]) for n in range(4)]
    ring_p1, ring_db, ring_p2, ring_da = rings
    count = tok_hbm.shape[0]
    block_rows, hidden = x.shape[2], x.shape[3]
    rows = BLOCKS * block_rows
    half = rows // 2
    width = w_out.shape[0]
    scale = head_dim ** -0.5
    masks = head_masks(width, head_dim)

    def x_in(s):
        slot = lax.rem(s, X_SLOTS)
        return pltpu.make_async_copy(tok_hbm.at[s], x.at[slot], x_sem.at[slot])

    def d_in(s):
        slot = lax.rem(s, D_SLOTS)
        return pltpu.make_async_copy(dout_hbm.at[s], d.at[slot], d_sem.at[slot])

    def out_copy(s):
        slot = lax.rem(s, SLOTS)
        return pltpu.make_async_copy(ring_p2.whole.at[slot], out_hbm.at[s], out_sem.at[slot])

    def dtok_copy(s):
        slot = lax.rem(s, SLOTS)
        return pltpu.make_async_copy(ring_da.whole.at[slot], dtok_hbm.at[s], dtok_sem.at[slot])

    def rows_sum(v):
        return jnp.sum(v.reshape(v.shape[0] // 8, 8, hidden), axis=0)

    def consume_p1(s):
        slot = lax.rem(s, SLOTS)

        def block(r):
            x1[slot, r] = (x[lax.rem(s, X_SLOTS), r].astype(F32) + ring_p1.whole[slot, r].astype(F32)).astype(BF16)
        loop(BLOCKS, block)

    def consume_p2(s):
        slot = lax.rem(s, SLOTS)

        def block(r):
            ring_p2.whole[slot, r] = (x1[slot, r].astype(F32) + ring_p2.whole[slot, r].astype(F32)).astype(BF16)
        loop(BLOCKS, block)
        out_copy(s).start()

    def consume_da(s):
        slot = lax.rem(s, SLOTS)

        def block(r):
            dx, dg = norm_back(x[lax.rem(s, X_SLOTS), r].astype(F32), gain_attn[...], ring_da.whole[slot, r].astype(F32))
            dg_attn[...] += rows_sum(dg)
            ring_da.whole[slot, r] = (d[lax.rem(s, D_SLOTS), r].astype(F32) + dx).astype(BF16)
        loop(BLOCKS, block)
        dtok_copy(s).start()

    def store_part(ring, slot, h, value):
        ring.part[slot, h * HALF:(h + 1) * HALF] = value.astype(BF16).reshape(HALF, block_rows, hidden)

    def norm_in(s):
        x_in(s).wait()

        def block(r):
            unit, _ = norm_stats(x[lax.rem(s, X_SLOTS), r].astype(F32))
            a[lax.rem(s, A_SLOTS), r] = (unit * gain_attn[...]).astype(BF16)
        loop(BLOCKS, block)
        slot = lax.rem(s, A_SLOTS)
        saved[slot, :, :3 * width] = mm(a[slot].reshape(rows, hidden), w_qkv[...]).astype(BF16)

    def attend(s):
        slot = lax.rem(s, A_SLOTS)

        def q_block(i):
            row0 = pl.multiple_of(i * Q_ROWS, Q_ROWS)
            part_rows = pl.ds(row0, Q_ROWS)
            q = saved[slot, part_rows, 0:width]
            k = saved[slot, :, width:2 * width]
            v = saved[slot, :, 2 * width:3 * width]
            out = None
            for mask in masks:
                p = probs_of(jnp.where(mask, q, 0).astype(BF16), k, seg_col[s, part_rows], seg_row[s], row0, scale)
                head = mm(p.astype(BF16), v)
                out = head if out is None else jnp.where(mask, head, out)
            saved[slot, part_rows, 3 * width:4 * width] = out.astype(BF16)
        loop(rows // Q_ROWS, q_block)

    def project(s):
        for h in range(2):
            proj = mm(saved[lax.rem(s, A_SLOTS), h * half:(h + 1) * half, 3 * width:4 * width], w_out[...])
            store_part(ring_p1, lax.rem(s, SLOTS), h, proj)
        ring_p1.stage(0, s)

    def norm_mid(s):
        def block(r):
            unit, _ = norm_stats(x1[lax.rem(s, SLOTS), r].astype(F32))
            b[r] = (unit * gain_mlp[...]).astype(BF16)
        loop(BLOCKS, block)
        d_in(s).wait()

    def up(s):
        pre[...] = mm(b[...].reshape(rows, hidden), w_up[...])
        d_hid[...] = mt(d[lax.rem(s, D_SLOTS)].reshape(rows, hidden), w_down[...])

    def gelu_both(s):
        def block(r):
            part_rows = pl.ds(pl.multiple_of(r * block_rows, block_rows), block_rows)
            v = pre[part_rows]
            v2 = v * v
            c = 0.7978845608028654
            th = jnp.tanh(c * (v + 0.044715 * (v * v2)))
            u[part_rows] = (0.5 * v * (1.0 + th)).astype(BF16)
            slope = 0.5 * (1.0 + th) + 0.5 * v * (1.0 - th * th) * (c * (1.0 + 3.0 * 0.044715 * v2))
            d_pre[part_rows] = (d_hid[part_rows].astype(BF16).astype(F32) * slope).astype(BF16)
        loop(BLOCKS, block)

    def grad_b(s):
        for h in range(2):
            store_part(ring_db, lax.rem(s, SLOTS), h, mt(d_pre[h * half:(h + 1) * half], w_up[...]))
        ring_db.stage(0, s)

    def down(s):
        @pl.when(s >= SLOTS)
        def _():
            out_copy(s - SLOTS).wait()
        for h in range(2):
            store_part(ring_p2, lax.rem(s, SLOTS), h, mm(u[h * half:(h + 1) * half], w_down[...]))
        ring_p2.stage(0, s)
        dw_up[...] += tm(b[...].reshape(rows, hidden), d_pre[...])
        dw_down[...] += tm(u[...], d[lax.rem(s, D_SLOTS)].reshape(rows, hidden))

    def grad_mid(s):
        slot = lax.rem(s, SLOTS)
        d_slot = lax.rem(s, D_SLOTS)

        def block(r):
            dx, dg = norm_back(x1[slot, r].astype(F32), gain_mlp[...], ring_db.whole[slot, r].astype(F32))
            dg_mlp[...] += rows_sum(dg)
            d[d_slot, r] = (d[d_slot, r].astype(F32) + dx).astype(BF16)
        loop(BLOCKS, block)
        d_rows = d[d_slot].reshape(rows, hidden)
        d_heads[...] = mt(d_rows, w_out[...]).astype(BF16)
        dw_out[...] += tm(saved[lax.rem(s, A_SLOTS), :, 3 * width:4 * width], d_rows)

    def attend_back(h, s):
        mask = masks[h]
        slot = lax.rem(s, A_SLOTS)

        def q_block(i):
            row0 = pl.multiple_of(i * Q_ROWS, Q_ROWS)
            part_rows = pl.ds(row0, Q_ROWS)
            q = jnp.where(mask, saved[slot, part_rows, 0:width], 0).astype(BF16)
            d_head = jnp.where(mask, d_heads[part_rows], 0).astype(BF16)
            p = probs_of(q, saved[slot, :, width:2 * width], seg_col[s, part_rows], seg_row[s], row0, scale)
            d_p = mt(d_head, saved[slot, :, 2 * width:3 * width])
            row_dot = jnp.sum(d_p * p, axis=-1, keepdims=True)
            probs[part_rows] = p.astype(BF16)
            d_scores[part_rows] = (p * (d_p - row_dot) * scale).astype(BF16)
        loop(rows // Q_ROWS, q_block)
        d_q = mm(d_scores[...], saved[slot, :, width:2 * width]).astype(BF16)
        d_k = tm(d_scores[...], saved[slot, :, 0:width]).astype(BF16)
        d_v = tm(probs[...], d_heads[...]).astype(BF16)
        for j, value in enumerate((d_q, d_k, d_v)):
            cols = slice(j * width, (j + 1) * width)
            d_qkv[:, cols] = value if h == 0 else jnp.where(mask, value, d_qkv[:, cols])

    def grad_a(s):
        @pl.when(s >= SLOTS)
        def _():
            dtok_copy(s - SLOTS).wait()
        for h in range(2):
            store_part(ring_da, lax.rem(s, SLOTS), h, mt(d_qkv[h * half:(h + 1) * half], w_qkv[...]))
        ring_da.stage(0, s)
        dw_qkv[...] += tm(a[lax.rem(s, A_SLOTS)].reshape(rows, hidden), d_qkv[...])

    work = [(0, norm_in), (0, attend), (0, project),
            (1, norm_mid), (1, up), (1, gelu_both), (1, grad_b), (1, down),
            (2, grad_mid), (2, functools.partial(attend_back, 0)), (2, functools.partial(attend_back, 1)), (2, grad_a)]
    assert len(work) == POINTS
    progress = make_progress(count, POINTS, [
        (ring_p1, 0, 2, consume_p1), (ring_db, 1, 6, None), (ring_p2, 1, 7, consume_p2), (ring_da, 2, 11, consume_da)])

    x_in(0).start()
    enter(size)
    for ref in (dw_qkv, dw_out, dw_up, dw_down, dg_attn, dg_mlp):
        ref[...] = jnp.zeros_like(ref)

    def step(t):
        @pl.when(t + 1 < count)
        def _():
            x_in(t + 1).start()

        @pl.when(t < count)
        def _():
            d_in(t).start()
        for i, (lead, fn) in enumerate(work):
            s = t - lead

            @pl.when(jnp.logical_and(s >= 0, s < count))
            def _(fn=fn, s=s):
                fn(s)
            progress(t, i)

    loop(count + 3, step)
    for acc, out in ((dw_qkv, dw_qkv_out), (dw_out, dw_out_out), (dw_up, dw_up_out), (dw_down, dw_down_out)):
        out[...] = acc[...].astype(BF16)
    dg_attn_out[...] = jnp.sum(dg_attn[...], axis=0, keepdims=True)
    dg_mlp_out[...] = jnp.sum(dg_mlp[...], axis=0, keepdims=True)
    for s in range(count - SLOTS, count):
        out_copy(s).wait()
        dtok_copy(s).wait()


def ring_buffers(block_rows, hidden):
    return [
        pltpu.VMEM((SLOTS, BLOCKS, block_rows, hidden), BF16),
        pltpu.VMEM((SLOTS, HALF, block_rows, hidden), BF16),
        pltpu.VMEM((SLOTS, 2, block_rows, hidden), BF16),
        pltpu.VMEM((SLOTS, 2, PIECE, block_rows, hidden), BF16),
        pltpu.VMEM((SLOTS, BLOCKS, block_rows, hidden), BF16),
    ]


def ring_sems():
    return [pltpu.SemaphoreType.DMA((SLOTS, COPIES)), pltpu.SemaphoreType.DMA((SLOTS, COPIES))]


def run_kernel(kernel, ident, outs, out_vmem, args, in_vmem, scratch):
    def spec(in_vmem):
        return pl.BlockSpec(memory_space=pltpu.VMEM if in_vmem else pl.ANY)
    return pl.pallas_call(
        kernel,
        out_shape=[jax.ShapeDtypeStruct(s, t) for s, t in outs],
        in_specs=[spec(v) for v in in_vmem],
        out_specs=[spec(v) for v in out_vmem],
        scratch_shapes=scratch,
        compiler_params=pltpu.CompilerParams(collective_id=ident, has_side_effects=True, vmem_limit_bytes=VMEM_LIMIT),
        name=f'layer_part_{ident}',
    )(*args)


def solution(mesh):
    size = mesh.shape['model']
    dma = pltpu.SemaphoreType.DMA

    def device_step(tokens, seg_ids, d_out, gain_attn, gain_mlp, w_qkv, w_out, w_up, w_down):
        count, seq_len, hidden = tokens.shape
        heads, head_dim = w_qkv.shape[1], w_qkv.shape[3]
        width = heads * head_dim
        inner = w_up.shape[1]
        block_rows = seq_len // BLOCKS
        act = (count, BLOCKS, block_rows, hidden)
        one = (BLOCKS, block_rows, hidden)
        x = tokens.reshape(act)
        d = d_out.reshape(act)
        seg_row = seg_ids.reshape(count, 1, seq_len)
        seg_col = seg_ids.reshape(count, seq_len, 1)
        g_attn = gain_attn.astype(F32).reshape(1, hidden)
        g_mlp = gain_mlp.astype(F32).reshape(1, hidden)
        wqkv = w_qkv.transpose(0, 2, 1, 3).reshape(hidden, 3 * width)
        wout = w_out.reshape(width, hidden)

        outs = [(act, BF16), (act, BF16), ((hidden, 3 * width), BF16), ((width, hidden), BF16),
                ((hidden, inner), BF16), ((inner, hidden), BF16), ((1, hidden), F32), ((1, hidden), F32)]
        scratch = [pltpu.VMEM(shape, kind) for shape, kind in (
            ((X_SLOTS,) + one, BF16), ((D_SLOTS,) + one, BF16), ((SLOTS,) + one, BF16), ((A_SLOTS,) + one, BF16),
            ((A_SLOTS, seq_len, 4 * width), BF16), (one, BF16), ((seq_len, inner), F32), ((seq_len, inner), F32),
            ((seq_len, inner), BF16), ((seq_len, inner), BF16), ((seq_len, width), BF16),
            ((seq_len, seq_len), BF16), ((seq_len, seq_len), BF16), ((seq_len, 3 * width), BF16),
            ((hidden, 3 * width), F32), ((width, hidden), F32), ((hidden, inner), F32), ((inner, hidden), F32),
            ((8, hidden), F32), ((8, hidden), F32))]
        scratch += [dma((X_SLOTS,)), dma((D_SLOTS,)), dma((SLOTS,)), dma((SLOTS,))]
        for _ in range(4):
            scratch += ring_buffers(block_rows, hidden) + ring_sems()
        layer_out, d_tokens, dw_qkv, dw_out, d_w_up, d_w_down, dg_attn, dg_mlp = run_kernel(
            functools.partial(layer_kernel, size, head_dim), 1, outs, [False] * 2 + [True] * 6,
            [x, d, seg_row, seg_col, g_attn, g_mlp, wqkv, wout, w_up, w_down], [False] * 2 + [True] * 8, scratch)

        d_w_qkv = dw_qkv.reshape(hidden, 3, heads, head_dim).transpose(0, 2, 1, 3)
        return (layer_out.reshape(tokens.shape), d_tokens.reshape(tokens.shape), d_w_qkv,
                dw_out.reshape(w_out.shape), d_w_up, d_w_down, dg_attn.reshape(hidden), dg_mlp.reshape(hidden))

    in_specs = (P('data', None, None), P('data', None), P('data', None, None), P(), P(), P(None, 'model', None, None), P('model', None, None), P(None, 'model'), P('model', None))
    out_specs = (P('data', None, None), P('data', None, None), P('data', 'model', None, None), P(('data', 'model'), None, None), P('data', 'model'), P(('data', 'model'), None), P('data'), P('data'))
    return jax.shard_map(device_step, mesh=mesh, in_specs=in_specs, out_specs=out_specs, check_vma=False)
```

time: 809 us -> 449 us (0.56)
  waiting for transfers between devices: 460 us -> 0 us
  Pallas kernels: 0 us -> 418 us
  matrix products: 202 us -> 0 us
  other arithmetic: 113 us -> 2.55 us
  local copies, waits for them, and re-layouts: 11.6 us -> 28.2 us
  between operations: 14.9 us -> 0.67 us
    psum x5 -> x0, waiting for transfers between devices: 460 us -> none  [the longest x2 198 us: forward_pass(): reduce_sum(jnp.einsum('bnsd,ndh->bsh', attn_heads, w_out, preferred_eleme...]
    pallas_call x0 -> x1, Pallas kernels: none -> 418 us  [run_kernel(): pl.pallas_call(kernel, out_shape=[jax.ShapeDtypeStruct(s, t) for s, t in...]
    dot_general x19 -> x0, matrix products: 179 us -> none  [the longest x1 23.6 us: backward_pass(): jnp.einsum('bnqk,bnqd->bnkd', d_scores, qkv_all[0], preferred_element_typ...]
    reduce_sum x12 -> x0, other arithmetic: 81.6 us -> none  [the longest x4 43.3 us: layer_norm(): return centered * lax.rsqrt(var_val + NORM_EPS) * gain_vec]
    convert_element_type x5 -> x0, other arithmetic: 29.1 us -> none  [the longest x1 10.6 us: forward_pass(): layer_out = (resid_f32 + mlp_down.astype(jnp.float32)).astype(jnp.bfloat16)]
    sub x2 -> x0, matrix products: 22.5 us -> none  [forward_pass(): attn_probs = jax.nn.softmax(jnp.where(allowed, scores, -1e+30), axis=-1)]
    unnamed x81 -> x19, local copies, waits for them, and re-layouts: 11.6 us -> 21.6 us
  transfers between devices with their start and end apart: 5 -> 0, of which waited for: 5 -> 0; matrix products, arithmetic and copies ran while one was open for 4% -> 0% of each run, Pallas kernels for 0% -> 0%
where the time goes in v2:
time: 449 us
  Pallas kernels  418 us (93%)
  local copies, waits for them, and re-layouts  28.2 us (6%)
    pallas_call x1, Pallas kernels, run_kernel(): pl.pallas_call(kernel, out_shape=[jax.ShapeDtypeStruct(s, t) for s, t in...  418 us
    unnamed x19, local copies, waits for them, and re-layouts  21.6 us

profile of v2, /device:TPU:81, one launch (start us, length us, event | category | flops | bytes accessed | tf_op | source)
XLA Modules:
  0.0 449.1 jit_solution(14104538052751049805)
XLA Ops:
  0.6 1.3 reshape.78
  1.9 1.3 reshape.80
  3.2 1.3 reshape.64.refs_2_
  4.5 1.2 copy.19
  5.7 1.2 copy.21.refs_6_
  6.9 2.7 copy.20.refs_3_
  9.5 417.6 %layer_part_1.1 = (bf16[8,16,32,1024]{3,2,1,0:T(8,128)(2,1)}, bf16[8,16,32,1024]{3,2,1,0:T(8,128)(2,1)}, bf16[1024,384]{1,0:T(8,128)(2,1)}, bf16[128,1024]{1,0:T...) custom-call(bf16[8,16,32,1024]{3,2,1,0:T(8,128)(2,1)} %bitcast.17, ...), custom_call_target="tpu_custom_call" | custom-call | tf_op jit(solution)/shard_map/layer_part_1/pallas_call | solution.py:438
  427.2 1.4 copy.22
  428.6 0.9 copy.23
  429.5 7.8 %copy.31 = bf16[8,512,1024]{2,1,0:T(8,128)(2,1)} copy(bf16[8,512,1024]{2,1,0:T(8,128)(2,1)} %bitcast.20) | data formatting | bytes 16777216
  437.3 0.0 copy-start.2
  437.3 0.0 copy-start.1
  437.3 0.0 copy-start
  437.3 0.0 copy-start.4
  437.3 0.0 copy-start.3
  437.3 7.9 %copy.32 = bf16[8,512,1024]{2,1,0:T(8,128)(2,1)} copy(bf16[8,512,1024]{2,1,0:T(8,128)(2,1)} %bitcast.19) | data formatting | bytes 16777216
  445.2 0.0 copy-done.2
  445.2 0.7 copy.33
  445.9 0.0 copy-done.1
  445.9 1.0 copy.34
  446.9 0.0 copy-done
  446.9 1.0 copy.35
  447.9 0.0 copy-done.4
  447.9 0.6 copy.36
  448.5 0.0 copy-done.3
  448.5 0.6 copy.37
Async XLA Ops:
  437.3 7.9 %copy-start.2 = (bf16[128,1024]{1,0:T(8,128)(2,1)S(1)}, bf16[128,1024]{1,0:T(8,128)(2,1)}, u32[]{:S(2)}) copy-start(bf16[128,1024]{1,0:T(8,128)(2,1)} %get-tuple-element.19) | copy-start | bytes 786436
  437.3 8.6 %copy-start.1 = (bf16[1024,512]{1,0:T(8,128)(2,1)S(1)}, bf16[1024,512]{1,0:T(8,128)(2,1)}, u32[]{:S(2)}) copy-start(bf16[1024,512]{1,0:T(8,128)(2,1)} %get-tuple-element.44) | copy-start | bytes 3145732
  437.3 9.6 %copy-start = (bf16[512,1024]{1,0:T(8,128)(2,1)S(1)}, bf16[512,1024]{1,0:T(8,128)(2,1)}, u32[]{:S(2)}) copy-start(bf16[512,1024]{1,0:T(8,128)(2,1)} %get-tuple-element.45) | copy-start | bytes 3145732
  437.3 10.6 %copy-start.4 = (f32[1,1024]{1,0:T(1,128)S(1)}, f32[1,1024]{1,0:T(1,128)}, u32[]{:S(2)}) copy-start(f32[1,1024]{1,0:T(1,128)} %get-tuple-element.22) | copy-start | bytes 12292
  437.3 11.2 %copy-start.3 = (f32[1,1024]{1,0:T(1,128)S(1)}, f32[1,1024]{1,0:T(1,128)}, u32[]{:S(2)}) copy-start(f32[1,1024]{1,0:T(1,128)} %get-tuple-element.23) | copy-start | bytes 12292

commit v3 on v2

v3 whole, which is shorter than its diff:
```python
import functools
import jax
import jax.numpy as jnp
from jax import lax
from jax.experimental import pallas as pl
from jax.experimental.pallas import tpu as pltpu
from jax.sharding import PartitionSpec as P

NORM_EPS = 1e-5
MESH = pl.DeviceIdType.MESH
F32 = jnp.float32
BF16 = jnp.bfloat16
SLOTS = 2
BLOCKS = 16
HALF = BLOCKS // 2
PIECE = 2
COPIES = 13
VMEM_LIMIT = 66 * 1000 * 1000


def mm(a, b):
    return lax.dot_general(a, b, (((1,), (0,)), ((), ())), preferred_element_type=F32)


def mt(a, b):
    return lax.dot_general(a, b, (((1,), (1,)), ((), ())), preferred_element_type=F32)


def tm(a, b):
    return lax.dot_general(a, b, (((0,), (0,)), ((), ())), preferred_element_type=F32)


def loop(count, body):
    def step(i, carry):
        body(i)
        return carry
    lax.fori_loop(0, count, step, 0)


class Gather:
    first, last = 0, 3

    def __init__(self, size, slots, view, send, recv):
        me = lax.axis_index('model')
        self.core = lax.rem(me, 2)
        self.chips = size // 2
        self.chip = me // 2
        self.right = lax.rem(me + 2, size)
        self.left = lax.rem(me + size - 2, size)
        self.partner = me + 1 - 2 * self.core
        self.slots, self.view, self.send, self.recv = slots, view, send, recv

    def at(self, slot, step, part=None):
        return self.view(slot, self.core, lax.rem(self.chip + step, self.chips), part)

    def remote(self, slot, n, src, dst, to):
        return pltpu.make_async_remote_copy(
            src_ref=src, dst_ref=dst, send_sem=self.send.at[slot, n], recv_sem=self.recv.at[slot, n],
            device_id={'model': to}, device_id_type=MESH)

    def copy(self, n, s):
        slot = lax.rem(s, self.slots)
        behind = self.chips - 1
        step, part, to = [(0, None, self.right), (0, None, self.left), (0, None, self.partner),
                          (behind, 0, self.right), (1, 1, self.left), (behind, None, self.partner),
                          (1, None, self.partner), (2, None, self.partner)][n]
        ref = self.at(slot, step, part)
        return self.remote(slot, n, ref, ref, to)

    def gather_stage(self, j, s):
        if j == 0:
            starts, waits = (0, 1, 2), ()
        elif j == 1:
            starts, waits = (3, 4, 5, 6), (0, 1)
        elif j == 2:
            starts, waits = (7,), (3, 4)
        else:
            starts, waits = (), (2, 5, 6, 7)
        for n in waits:
            self.copy(n, s).wait_recv()
        for n in starts:
            self.copy(n, s).start()
        if j == 3:
            for n in range(8):
                self.copy(n, s).wait_send()

    def stage(self, j, s):
        self.gather_stage(j, s)


class RingSum(Gather):
    last = 6

    def __init__(self, size, part, pair_in, relay_in, ring_in, whole, send, recv):
        self.part, self.pair_in, self.relay_in, self.ring_in, self.whole = part, pair_in, relay_in, ring_in, whole
        super().__init__(size, SLOTS, self.block_view, send, recv)

    def block_view(self, slot, core, chip, part):
        start = core * HALF + chip * PIECE
        if part is None:
            return self.whole.at[slot, pl.ds(start, PIECE)]
        return self.whole.at[slot, pl.ds(start + part, 1)]

    def base(self, step):
        return self.core * HALF + lax.rem(self.chip + step, self.chips) * PIECE

    def sum_copy(self, n, s):
        slot = lax.rem(s, SLOTS)
        part = self.part.at[slot]
        if n == 8:
            src, dst, to = part.at[pl.ds((1 - self.core) * HALF, HALF)], self.pair_in.at[slot], self.partner
        elif n == 9:
            src, dst, to = part.at[pl.ds(self.base(2), 1)], self.relay_in.at[slot, pl.ds(0, 1)], self.right
        elif n == 10:
            src, dst, to = part.at[pl.ds(self.base(2) + 1, 1)], self.relay_in.at[slot, pl.ds(1, 1)], self.left
        elif n == 11:
            src, dst, to = part.at[pl.ds(self.base(1), PIECE)], self.ring_in.at[slot, 0], self.right
        else:
            src, dst, to = part.at[pl.ds(self.base(self.chips - 1), PIECE)], self.ring_in.at[slot, 1], self.left
        return self.remote(slot, n, src, dst, to)

    def add(self, slot, block, others):
        total = self.part[slot, block].astype(F32)
        for ref in others:
            total = total + ref.astype(F32)
        return total.astype(BF16)

    def stage(self, j, s):
        slot = lax.rem(s, SLOTS)
        if j == 0:
            self.sum_copy(8, s).start()
        elif j == 1:
            self.sum_copy(8, s).wait_recv()

            def pair(i):
                at = lax.rem(lax.rem(self.chip + 2, self.chips) * PIECE + i, HALF)
                block = self.core * HALF + at
                self.part[slot, block] = self.add(slot, block, [self.pair_in[slot, at]])
            loop(HALF, pair)
            self.sum_copy(9, s).start()
            self.sum_copy(10, s).start()
        elif j == 2:
            self.sum_copy(9, s).wait_recv()
            self.sum_copy(10, s).wait_recv()
            first, second = self.base(1), self.base(self.chips - 1) + 1
            self.part[slot, first] = self.add(slot, first, [self.relay_in[slot, 0]])
            self.part[slot, second] = self.add(slot, second, [self.relay_in[slot, 1]])
            self.sum_copy(11, s).start()
            self.sum_copy(12, s).start()
        elif j == 3:
            self.sum_copy(11, s).wait_recv()
            self.sum_copy(12, s).wait_recv()
            for i in range(PIECE):
                block = self.base(0) + i
                self.whole[slot, block] = self.add(slot, block, [self.ring_in[slot, 0, i], self.ring_in[slot, 1, i]])
            self.gather_stage(0, s)
        else:
            self.gather_stage(j - 3, s)
            if j == self.last:
                for n in range(8, COPIES):
                    self.sum_copy(n, s).wait_send()


def enter(size):
    me = lax.axis_index('model')
    barrier = pltpu.get_barrier_semaphore()
    for other in (lax.rem(me + 2, size), lax.rem(me + size - 2, size), me + 1 - 2 * lax.rem(me, 2)):
        pl.semaphore_signal(barrier, inc=1, device_id={'model': other}, device_id_type=MESH)
    pl.semaphore_wait(barrier, 3)


def make_progress(points, sums):
    def progress(t, i):
        for ring, count, lead, start, offsets, consume in sums:
            for j in range(ring.last, 0, -1):
                ahead = start + offsets[j - 1] - i
                if ahead % points:
                    continue
                s = t - lead - ahead // points

                @pl.when(jnp.logical_and(s >= 0, s < count))
                def _(ring=ring, consume=consume, j=j, s=s):
                    ring.stage(j, s)
                    if j == ring.last and consume is not None:
                        consume(s)
    return progress


def norm_stats(x):
    mean = jnp.mean(x, axis=-1, keepdims=True)
    centered = x - mean
    var = jnp.mean(centered * centered, axis=-1, keepdims=True)
    inv = lax.rsqrt(var + NORM_EPS)
    return centered * inv, inv


def norm_back(x, gain, d_normed):
    unit, inv = norm_stats(x)
    d_unit = d_normed * gain
    mean_d = jnp.mean(d_unit, axis=-1, keepdims=True)
    mean_du = jnp.mean(d_unit * unit, axis=-1, keepdims=True)
    return inv * (d_unit - mean_d - unit * mean_du), d_normed * unit


def probs_of(q, k, seg_ref, s, row0, scale):
    keys = k.shape[0]
    seg_q = seg_ref[s, :, pl.ds(row0, Q_ROWS)]
    seg_q = jnp.broadcast_to(seg_q, (Q_ROWS, Q_ROWS)).T[:, :1]
    seg_k = seg_ref[s, :, :keys]
    scores = mt(q, k) * scale
    q_pos = row0 + lax.broadcasted_iota(jnp.int32, scores.shape, 0)
    k_pos = lax.broadcasted_iota(jnp.int32, scores.shape, 1)
    allowed = jnp.logical_and(seg_q == seg_k, q_pos >= k_pos)
    scores = jnp.where(allowed, scores, -1e30)
    e = jnp.exp(scores - jnp.max(scores, axis=-1, keepdims=True))
    return e * (1.0 / jnp.sum(e, axis=-1, keepdims=True))


def head_masks(width, head_dim):
    lane = lax.broadcasted_iota(jnp.int32, (1, width), 1)
    return [jnp.logical_and(lane >= h * head_dim, lane < (h + 1) * head_dim) for h in range(width // head_dim)]


Q_ROWS = 128

ORDER = ['A0', 'A1', 'A2', 'B0', 'B1', 'A3', 'B2', 'B3', 'B4', 'B5', 'B6', 'C0', 'C1', 'C2', 'B7', 'C3', 'C4', 'C5',
         'C6', 'C7', 'B8', 'C8']
STAGES = {'p1': [7, 18, 19], 'db': [1, 6, 12, 16, 22, 23], 'p2': [7, 13, 20, 31, 34, 35], 'da': [1, 7, 17, 25, 31, 32]}
STARTS = {'p1': 'A3', 'db': 'B5', 'p2': 'B6', 'da': 'C7'}


class Plan:
    def __init__(self):
        self.points = n = len(ORDER)
        self.pos = {tag: i for i, tag in enumerate(ORDER)}
        self.start = {ring: self.pos[tag] for ring, tag in STARTS.items()}
        self.lead = {'A': 0}
        self.lead['B'] = self.after('p1', 'B0')
        self.lead['C'] = self.after('db', 'C0')
        end = {ring: self.end(ring) // n for ring in STAGES}
        self.steps = max(end.values())
        self.x_slots = end['da'] + 2
        self.d_slots = end['da'] - self.lead['B'] + 1
        self.x1_slots = max(self.lead['C'], end['p2']) - end['p1'] + 1
        self.a_slots = self.lead['C'] + 1
        self.head_slots = 2 if STAGES['p1'][-1] < n else 3
        assert all(o[-1] < 2 * n for o in STAGES.values())
        assert self.lead['C'] * n + self.pos['C1'] < (self.lead['B'] + 2) * n + self.start['db']

    def ring_lead(self, ring):
        return self.lead[STARTS[ring][0]]

    def end(self, ring):
        return self.ring_lead(ring) * self.points + self.start[ring] + STAGES[ring][-1]

    def after(self, ring, tag):
        end = self.end(ring)
        return end // self.points + (0 if self.pos[tag] > end % self.points else 1)


def layer_kernel(size, head_dim, plan, *refs):
    (tok_hbm, dout_hbm, seg_in, gains, w_qkv_in, w_out, w_up, w_down,
     out_hbm, dtok_hbm, dw_qkv_out, dw_out_out, dw_up_out, dw_down_out, dg_out,
     x, d, x1, a, saved, heads, w_qkv, w_out_all, b, pre, d_hid, u, d_pre, d_heads, probs, d_scores, d_qkv,
     dw_qkv, dw_out, dw_up, dw_down, dg_attn, dg_mlp,
     seg, x_sem, d_sem, out_sem, dtok_sem, heads_send, heads_recv, wout_send, wout_recv) = refs[:47]
    ring_db, ring_p2, ring_da = [RingSum(size, *refs[47 + 7 * n:54 + 7 * n]) for n in range(3)]
    count = tok_hbm.shape[0]
    block_rows, hidden = x.shape[2], x.shape[3]
    rows = BLOCKS * block_rows
    half = rows // 2
    width = w_out.shape[0]
    scale = head_dim ** -0.5
    masks = head_masks(width, head_dim)
    me = lax.axis_index('model')
    my_lanes = pl.ds(pl.multiple_of(me * width, width), width)
    gain_attn, gain_mlp = gains.at[0:1], gains.at[1:2]

    def heads_view(slot, core, chip, part):
        lanes = pl.ds(pl.multiple_of((2 * chip + core) * width, width), width)
        span = pl.ds(0, rows) if part is None else pl.ds(part * half, half)
        return heads.at[slot, span, lanes]

    def wout_view(slot, core, chip, part):
        first = (2 * chip + core) * width
        if part is None:
            return w_out_all.at[pl.ds(pl.multiple_of(first, width), width)]
        size_half = width // 2
        return w_out_all.at[pl.ds(pl.multiple_of(first + part * size_half, size_half), size_half)]

    gather_p1 = Gather(size, plan.head_slots, heads_view, heads_send, heads_recv)
    gather_wout = Gather(size, 1, wout_view, wout_send, wout_recv)

    def x_in(s):
        slot = lax.rem(s, plan.x_slots)
        return pltpu.make_async_copy(tok_hbm.at[s], x.at[slot], x_sem.at[slot])

    def d_in(s):
        slot = lax.rem(s, plan.d_slots)
        return pltpu.make_async_copy(dout_hbm.at[s], d.at[slot], d_sem.at[slot])

    def out_copy(s):
        slot = lax.rem(s, SLOTS)
        return pltpu.make_async_copy(ring_p2.whole.at[slot], out_hbm.at[s], out_sem.at[slot])

    def dtok_copy(s):
        slot = lax.rem(s, SLOTS)
        return pltpu.make_async_copy(ring_da.whole.at[slot], dtok_hbm.at[s], dtok_sem.at[slot])

    def rows_sum(v):
        return jnp.sum(v.reshape(v.shape[0] // 8, 8, hidden), axis=0)

    def consume_p1(s):
        x_slot, x1_slot, h_slot = lax.rem(s, plan.x_slots), lax.rem(s, plan.x1_slots), lax.rem(s, plan.head_slots)
        for h in range(2):
            blocks = slice(h * HALF, (h + 1) * HALF)
            proj = mm(heads[h_slot, h * half:(h + 1) * half], w_out_all[...]).astype(BF16).reshape(HALF, block_rows, hidden)
            x1[x1_slot, blocks] = (x[x_slot, blocks].astype(F32) + proj.astype(F32)).astype(BF16)

    def consume_p2(s):
        slot, x1_slot = lax.rem(s, SLOTS), lax.rem(s, plan.x1_slots)

        def block(r):
            ring_p2.whole[slot, r] = (x1[x1_slot, r].astype(F32) + ring_p2.whole[slot, r].astype(F32)).astype(BF16)
        loop(BLOCKS, block)
        out_copy(s).start()

    def consume_da(s):
        slot, x_slot, d_slot = lax.rem(s, SLOTS), lax.rem(s, plan.x_slots), lax.rem(s, plan.d_slots)

        def block(r):
            dx, dg = norm_back(x[x_slot, r].astype(F32), gain_attn[...], ring_da.whole[slot, r].astype(F32))
            dg_attn[...] += rows_sum(dg)
            ring_da.whole[slot, r] = (d[d_slot, r].astype(F32) + dx).astype(BF16)
        loop(BLOCKS, block)
        dtok_copy(s).start()

    def store_part(ring, slot, h, value):
        ring.part[slot, h * HALF:(h + 1) * HALF] = value.astype(BF16).reshape(HALF, block_rows, hidden)

    def norm_in(h, s):
        x_slot, slot = lax.rem(s, plan.x_slots), lax.rem(s, plan.a_slots)
        if h == 0:
            x_in(s).wait()

        def block(i):
            r = h * HALF + i
            unit, _ = norm_stats(x[x_slot, r].astype(F32))
            a[slot, r] = (unit * gain_attn[...]).astype(BF16)
        loop(HALF, block)
        if h == 1:
            saved[slot, :, :3 * width] = mt(a[slot].reshape(rows, hidden), w_qkv[...]).astype(BF16)

    def attend(h, s):
        slot, h_slot = lax.rem(s, plan.a_slots), lax.rem(s, plan.head_slots)
        keys = (h + 1) * half

        def q_block(i):
            row0 = pl.multiple_of(h * half + i * Q_ROWS, Q_ROWS)
            part_rows = pl.ds(row0, Q_ROWS)
            q = saved[slot, part_rows, 0:width]
            k = saved[slot, :keys, width:2 * width]
            v = saved[slot, :keys, 2 * width:3 * width]
            out = None
            for mask in masks:
                p = probs_of(jnp.where(mask, q, 0).astype(BF16), k, seg, s, row0, scale)
                head = mm(p.astype(BF16), v)
                out = head if out is None else jnp.where(mask, head, out)
            out = out.astype(BF16)
            saved[slot, part_rows, 3 * width:4 * width] = out
            heads[h_slot, part_rows, my_lanes] = out
        loop(half // Q_ROWS, q_block)
        if h == 1:
            gather_p1.stage(0, s)

    def norm_mid(h, s):
        x1_slot = lax.rem(s, plan.x1_slots)

        def block(i):
            r = h * HALF + i
            unit, _ = norm_stats(x1[x1_slot, r].astype(F32))
            b[r] = (unit * gain_mlp[...]).astype(BF16)
        loop(HALF, block)

    def up(s):
        pre[...] = mm(b[...].reshape(rows, hidden), w_up[...])

    def gelu_both(h, s):
        if h == 0:
            d_in(s).wait()
            d_hid[...] = mt(d[lax.rem(s, plan.d_slots)].reshape(rows, hidden), w_down[...]).astype(BF16)

        def block(i):
            part_rows = pl.ds(pl.multiple_of(h * half + i * block_rows, block_rows), block_rows)
            v = pre[part_rows]
            v2 = v * v
            c = 0.7978845608028654
            th = jnp.tanh(c * (v + 0.044715 * (v * v2)))
            u[part_rows] = (0.5 * v * (1.0 + th)).astype(BF16)
            slope = 0.5 * (1.0 + th) + 0.5 * v * (1.0 - th * th) * (c * (1.0 + 3.0 * 0.044715 * v2))
            d_pre[part_rows] = (d_hid[part_rows].astype(F32) * slope).astype(BF16)
        loop(HALF, block)

    def grad_b(s):
        for h in range(2):
            store_part(ring_db, lax.rem(s, SLOTS), h, mt(d_pre[h * half:(h + 1) * half], w_up[...]))
        ring_db.stage(0, s)

    def down(s):
        @pl.when(s >= SLOTS)
        def _():
            out_copy(s - SLOTS).wait()
        for h in range(2):
            store_part(ring_p2, lax.rem(s, SLOTS), h, mm(u[h * half:(h + 1) * half], w_down[...]))
        ring_p2.stage(0, s)

    def grad_up(s):
        dw_up[...] += tm(b[...].reshape(rows, hidden), d_pre[...])

    def grad_down(s):
        dw_down[...] += tm(u[...], d[lax.rem(s, plan.d_slots)].reshape(rows, hidden))

    def grad_mid(h, s):
        slot, x1_slot, d_slot = lax.rem(s, SLOTS), lax.rem(s, plan.x1_slots), lax.rem(s, plan.d_slots)

        def block(i):
            r = h * HALF + i
            dx, dg = norm_back(x1[x1_slot, r].astype(F32), gain_mlp[...], ring_db.whole[slot, r].astype(F32))
            dg_mlp[...] += rows_sum(dg)
            d[d_slot, r] = (d[d_slot, r].astype(F32) + dx).astype(BF16)
        loop(HALF, block)

    def grad_heads(s):
        d_rows = d[lax.rem(s, plan.d_slots)].reshape(rows, hidden)
        d_heads[...] = mt(d_rows, w_out[...]).astype(BF16)
        dw_out[...] += tm(saved[lax.rem(s, plan.a_slots), :, 3 * width:4 * width], d_rows)

    def attend_back(head, s):
        mask = masks[head]
        slot = lax.rem(s, plan.a_slots)
        for h in range(2):
            keys = (h + 1) * half

            def q_block(i):
                row0 = pl.multiple_of(h * half + i * Q_ROWS, Q_ROWS)
                part_rows = pl.ds(row0, Q_ROWS)
                q = jnp.where(mask, saved[slot, part_rows, 0:width], 0).astype(BF16)
                d_head = jnp.where(mask, d_heads[part_rows], 0).astype(BF16)
                p = probs_of(q, saved[slot, :keys, width:2 * width], seg, s, row0, scale)
                d_p = mt(d_head, saved[slot, :keys, 2 * width:3 * width])
                row_dot = jnp.sum(d_p * p, axis=-1, keepdims=True)
                probs[part_rows, :keys] = p.astype(BF16)
                d_scores[part_rows, :keys] = (p * (d_p - row_dot) * scale).astype(BF16)
            loop(half // Q_ROWS, q_block)

    def head_grads(head, s):
        mask = masks[head]
        slot = lax.rem(s, plan.a_slots)
        d_q = mm(d_scores[...], saved[slot, :, width:2 * width]).astype(BF16)
        d_k = tm(d_scores[...], saved[slot, :, 0:width]).astype(BF16)
        d_v = tm(probs[...], d_heads[...]).astype(BF16)
        for j, value in enumerate((d_q, d_k, d_v)):
            cols = slice(j * width, (j + 1) * width)
            d_qkv[:, cols] = value if head == 0 else jnp.where(mask, value, d_qkv[:, cols])

    def grad_a(s):
        @pl.when(s >= SLOTS)
        def _():
            dtok_copy(s - SLOTS).wait()
        for h in range(2):
            store_part(ring_da, lax.rem(s, SLOTS), h, mm(d_qkv[h * half:(h + 1) * half], w_qkv[...]))
        ring_da.stage(0, s)

    def grad_qkv(s):
        dw_qkv[...] += tm(d_qkv[...], a[lax.rem(s, plan.a_slots)].reshape(rows, hidden))

    def with_h(fn, h):
        return functools.partial(fn, h)

    work = {'A': [with_h(norm_in, 0), with_h(norm_in, 1), with_h(attend, 0), with_h(attend, 1)],
            'B': [with_h(norm_mid, 0), with_h(norm_mid, 1), up, with_h(gelu_both, 0), with_h(gelu_both, 1), grad_b, down,
                  grad_up, grad_down],
            'C': [with_h(grad_mid, 0), with_h(grad_mid, 1), grad_heads, with_h(attend_back, 0), with_h(head_grads, 0),
                  with_h(attend_back, 1), with_h(head_grads, 1), grad_a, grad_qkv]}
    assert sum(len(v) for v in work.values()) == plan.points
    first = plan.start['p1']
    progress = make_progress(plan.points, [(gather_wout, 1, 0, 0, [first + 1, first + 4, first + 7], None)] + [
        (ring, count, plan.ring_lead(name), plan.start[name], STAGES[name], consume) for name, ring, consume in (
            ('p1', gather_p1, consume_p1), ('db', ring_db, None), ('p2', ring_p2, consume_p2), ('da', ring_da, consume_da))])

    x_in(0).start()
    for s in range(count):
        seg[s] = seg_in[s:s + 1]
    w_out_all[my_rows(me, width)] = w_out[...]
    enter(size)
    gather_wout.stage(0, 0)
    for n in range(w_qkv_in.shape[0]):
        for j in range(3):
            at = (j * w_qkv_in.shape[0] + n) * head_dim
            w_qkv[at:at + head_dim] = w_qkv_in[n, j]
    for ref in (dw_qkv, dw_out, dw_up, dw_down, dg_attn, dg_mlp, probs, d_scores):
        ref[...] = jnp.zeros_like(ref)

    def step(t):
        @pl.when(t + 1 < count)
        def _():
            x_in(t + 1).start()
        s_mid = t - plan.lead['B']

        @pl.when(jnp.logical_and(s_mid >= 0, s_mid < count))
        def _():
            d_in(s_mid).start()
        for i, tag in enumerate(ORDER):
            s = t - plan.lead[tag[0]]

            @pl.when(jnp.logical_and(s >= 0, s < count))
            def _(fn=work[tag[0]][int(tag[1:])], s=s):
                fn(s)
            progress(t, i)

    loop(count + plan.steps, step)
    for acc, out in ((dw_out, dw_out_out), (dw_up, dw_up_out), (dw_down, dw_down_out)):
        out[...] = acc[...].astype(BF16)
    for n in range(w_qkv_in.shape[0]):
        for j in range(3):
            at = (j * w_qkv_in.shape[0] + n) * head_dim
            dw_qkv_out[n, j] = dw_qkv[at:at + head_dim].astype(BF16)
    dg_out[0:1] = jnp.sum(dg_attn[...], axis=0, keepdims=True)
    dg_out[1:2] = jnp.sum(dg_mlp[...], axis=0, keepdims=True)
    for s in range(count - SLOTS, count):
        out_copy(s).wait()
        dtok_copy(s).wait()


def my_rows(me, width):
    return pl.ds(pl.multiple_of(me * width, width), width)


def publish_kernel(count, *refs):
    n = len(refs) // 5
    ins, outs, held, in_sems, out_sems = (refs[k * n:(k + 1) * n] for k in range(5))

    def moves(i):
        if i >= count:
            yield (pltpu.make_async_copy(ins[i], held[i], in_sems[i].at[0]),
                   pltpu.make_async_copy(held[i], outs[i], out_sems[i].at[0]))
            return
        for r in range(ins[i].shape[0]):
            yield (pltpu.make_async_copy(ins[i].at[r], held[i].at[r], in_sems[i].at[r]),
                   pltpu.make_async_copy(held[i].at[r], outs[i].at[r], out_sems[i].at[r]))
    pairs = [pair for i in range(n) for pair in moves(i)]
    for into, _ in pairs:
        into.start()
    for into, out in pairs:
        into.wait()
        out.start()
    for _, out in pairs:
        out.wait()


def publish(values, split):
    sems = [pltpu.SemaphoreType.DMA((v.shape[0] if i < split else 1,)) for i, v in enumerate(values)]
    return pl.pallas_call(
        functools.partial(publish_kernel, split),
        out_shape=[jax.ShapeDtypeStruct(v.shape, v.dtype) for v in values],
        in_specs=[pl.BlockSpec(memory_space=pl.ANY)] * len(values),
        out_specs=[pl.BlockSpec(memory_space=pl.ANY)] * len(values),
        scratch_shapes=[pltpu.VMEM(v.shape, v.dtype) for v in values] + sems + sems,
        compiler_params=pltpu.CompilerParams(vmem_limit_bytes=VMEM_LIMIT),
        name='publish',
    )(*values)


def ring_buffers(block_rows, hidden):
    return [
        pltpu.VMEM((SLOTS, BLOCKS, block_rows, hidden), BF16),
        pltpu.VMEM((SLOTS, HALF, block_rows, hidden), BF16),
        pltpu.VMEM((SLOTS, 2, block_rows, hidden), BF16),
        pltpu.VMEM((SLOTS, 2, PIECE, block_rows, hidden), BF16),
        pltpu.VMEM((SLOTS, BLOCKS, block_rows, hidden), BF16),
    ]


def ring_sems():
    return [pltpu.SemaphoreType.DMA((SLOTS, COPIES)), pltpu.SemaphoreType.DMA((SLOTS, COPIES))]


def run_kernel(kernel, ident, outs, out_vmem, args, in_vmem, scratch):
    def spec(in_vmem):
        return pl.BlockSpec(memory_space=pltpu.VMEM if in_vmem else pl.ANY)
    return pl.pallas_call(
        kernel,
        out_shape=[jax.ShapeDtypeStruct(s, t) for s, t in outs],
        in_specs=[spec(v) for v in in_vmem],
        out_specs=[spec(v) for v in out_vmem],
        scratch_shapes=scratch,
        compiler_params=pltpu.CompilerParams(collective_id=ident, has_side_effects=True, vmem_limit_bytes=VMEM_LIMIT),
        name=f'layer_part_{ident}',
    )(*args)


def solution(mesh):
    size = mesh.shape['model']
    dma = pltpu.SemaphoreType.DMA

    def device_step(tokens, seg_ids, d_out, gain_attn, gain_mlp, w_qkv, w_out, w_up, w_down):
        count, seq_len, hidden = tokens.shape
        heads, head_dim = w_qkv.shape[1], w_qkv.shape[3]
        width = heads * head_dim
        inner = w_up.shape[1]
        block_rows = seq_len // BLOCKS
        act = (count, BLOCKS, block_rows, hidden)
        one = (BLOCKS, block_rows, hidden)
        x = tokens.reshape(act)
        d = d_out.reshape(act)
        gains = jnp.stack([gain_attn, gain_mlp]).astype(F32)
        wqkv = w_qkv.transpose(1, 2, 3, 0)
        wout = w_out.reshape(width, hidden)
        plan = Plan()

        outs = [(act, BF16), (act, BF16), (wqkv.shape, BF16), ((width, hidden), BF16),
                ((hidden, inner), BF16), ((inner, hidden), BF16), ((2, hidden), F32)]
        scratch = [pltpu.VMEM(shape, kind) for shape, kind in (
            ((plan.x_slots,) + one, BF16), ((plan.d_slots,) + one, BF16), ((plan.x1_slots,) + one, BF16),
            ((plan.a_slots,) + one, BF16), ((plan.a_slots, seq_len, 4 * width), BF16),
            ((plan.head_slots, seq_len, size * width), BF16), ((3 * width, hidden), BF16), ((size * width, hidden), BF16),
            (one, BF16), ((seq_len, inner), F32), ((seq_len, inner), BF16),
            ((seq_len, inner), BF16), ((seq_len, inner), BF16), ((seq_len, width), BF16),
            ((seq_len, seq_len), BF16), ((seq_len, seq_len), BF16), ((seq_len, 3 * width), BF16),
            ((3 * width, hidden), F32), ((width, hidden), F32), ((hidden, inner), F32), ((inner, hidden), F32),
            ((8, hidden), F32), ((8, hidden), F32), ((count, 1, seq_len), jnp.int32))]
        scratch += [dma((plan.x_slots,)), dma((plan.d_slots,)), dma((SLOTS,)), dma((SLOTS,))]
        scratch += [dma((plan.head_slots, 8))] * 2 + [dma((1, 8))] * 2
        for _ in range(3):
            scratch += ring_buffers(block_rows, hidden) + ring_sems()
        results = run_kernel(
            functools.partial(layer_kernel, size, head_dim, plan), 1, outs, [False] * 2 + [True] * 5,
            [x, d, seg_ids, gains, wqkv, wout, w_up, w_down], [False] * 2 + [True] * 6, scratch)
        layer_out, d_tokens, dw_qkv, dw_out, d_w_up, d_w_down, dg = publish(results, 2)

        return (layer_out.reshape(tokens.shape), d_tokens.reshape(tokens.shape), dw_qkv.transpose(3, 0, 1, 2),
                dw_out.reshape(w_out.shape), d_w_up, d_w_down, dg[0], dg[1])

    in_specs = (P('data', None, None), P('data', None), P('data', None, None), P(), P(), P(None, 'model', None, None), P('model', None, None), P(None, 'model'), P('model', None))
    out_specs = (P('data', None, None), P('data', None, None), P('data', 'model', None, None), P(('data', 'model'), None, None), P('data', 'model'), P(('data', 'model'), None), P('data'), P('data'))
    return jax.shard_map(device_step, mesh=mesh, in_specs=in_specs, out_specs=out_specs, check_vma=False)
```

time: 449 us -> 379 us (0.84)
  Pallas kernels: 418 us -> 375 us
  local copies, waits for them, and re-layouts: 28.2 us -> 2.75 us
    pallas_call x1, Pallas kernels: 418 us -> 362 us  [run_kernel(): pl.pallas_call(kernel, out_shape=[jax.ShapeDtypeStruct(s, t) for s, t in...]
    unnamed x19 -> x0, local copies, waits for them, and re-layouts: 21.6 us -> none
    pallas_call x0 -> x1, Pallas kernels: none -> 12.8 us  [publish(): pl.pallas_call(functools.partial(publish_kernel, split), out_shape=[jax.S...]
    reshape x3 -> x0, local copies, waits for them, and re-layouts: 5.17 us -> none  [the longest x1 2.68 us: device_step(): seg_col = seg_ids.reshape(count, seq_len, 1)]
where the time goes in v3:
time: 379 us
  Pallas kernels  375 us (99%)
    pallas_call x1, Pallas kernels, run_kernel(): pl.pallas_call(kernel, out_shape=[jax.ShapeDtypeStruct(s, t) for s, t in...  362 us
    pallas_call x1, Pallas kernels, publish(): pl.pallas_call(functools.partial(publish_kernel, split), out_shape=[jax.S...  12.8 us

profile of v3, /device:TPU:81, one launch (start us, length us, event | category | flops | bytes accessed | tf_op | source)
XLA Modules:
  0.0 378.7 jit_solution(12898121991389341533)
XLA Ops:
  0.6 0.7 stack.9
  1.3 0.7 stack.10
  2.0 0.6 maximum_convert_fusion.refs_3_
  2.6 361.9 %layer_part_1.1 = (bf16[8,16,32,1024]{3,2,1,0:T(8,128)(2,1)}, bf16[8,16,32,1024]{3,2,1,0:T(8,128)(2,1)}, bf16[2,3,64,1024]{3,2,1,0:T(8,128)(2,1)}, bf16[128,1024...) custom-call(bf16[8,16,32,1024]{3,2,1,0:T(8,128)(2,1)} %bitcast.10, ...), custom_call_target="tpu_custom_call" | custom-call | tf_op jit(solution)/shard_map/layer_part_1/pallas_call | solution.py:591
  364.5 12.8 %publish.1 = (bf16[8,16,32,1024]{3,2,1,0:T(8,128)(2,1)}, bf16[8,16,32,1024]{3,2,1,0:T(8,128)(2,1)}, bf16[2,3,64,1024]{3,2,1,0:T(8,128)(2,1)}, bf16[128,1024]{1,0...) custom-call(bf16[8,16,32,1024]{3,2,1,0:T(8,128)(2,1)} %get-tuple-element.22.refs_0_, ...), custom_call_target="tpu_custom_call" | custom-call | tf_op jit(solution)/shard_map/publish/pallas_call | solution.py:563
  377.3 1.4 fusion

commit v4 on v3

--- a/solution.py
+++ b/solution.py
@@ -223,10 +223,10 @@
 
 Q_ROWS = 128
 
-ORDER = ['A0', 'A1', 'A2', 'B0', 'B1', 'A3', 'B2', 'B3', 'B4', 'B5', 'B6', 'C0', 'C1', 'C2', 'B7', 'C3', 'C4', 'C5',
-         'C6', 'C7', 'B8', 'C8']
-STAGES = {'p1': [7, 18, 19], 'db': [1, 6, 12, 16, 22, 23], 'p2': [7, 13, 20, 31, 34, 35], 'da': [1, 7, 17, 25, 31, 32]}
-STARTS = {'p1': 'A3', 'db': 'B5', 'p2': 'B6', 'da': 'C7'}
+ORDER = ['A0', 'A1', 'B0', 'B1', 'B2', 'B3', 'B4', 'B5', 'B6', 'B7', 'A2', 'B8', 'C0', 'A3', 'C1', 'C2', 'C3', 'C4',
+         'C5', 'C6', 'C7', 'C8']
+STAGES = {'p1': [14, 25, 32], 'mlp': [1, 4, 13, 22, 24, 25], 'da': [3, 10, 13, 21, 26, 34]}
+STARTS = {'p1': 'A3', 'mlp': 'B6', 'da': 'C7'}
 
 
 class Plan:
@@ -236,16 +236,16 @@
         self.start = {ring: self.pos[tag] for ring, tag in STARTS.items()}
         self.lead = {'A': 0}
         self.lead['B'] = self.after('p1', 'B0')
-        self.lead['C'] = self.after('db', 'C0')
+        self.lead['C'] = self.after('mlp', 'C0')
         end = {ring: self.end(ring) // n for ring in STAGES}
         self.steps = max(end.values())
         self.x_slots = end['da'] + 2
         self.d_slots = end['da'] - self.lead['B'] + 1
-        self.x1_slots = max(self.lead['C'], end['p2']) - end['p1'] + 1
+        self.x1_slots = max(self.lead['C'], end['mlp']) - end['p1'] + 1
         self.a_slots = self.lead['C'] + 1
         self.head_slots = 2 if STAGES['p1'][-1] < n else 3
         assert all(o[-1] < 2 * n for o in STAGES.values())
-        assert self.lead['C'] * n + self.pos['C1'] < (self.lead['B'] + 2) * n + self.start['db']
+        assert self.lead['C'] * n + self.pos['C1'] < (self.lead['B'] + 2) * n + self.start['mlp']
 
     def ring_lead(self, ring):
         return self.lead[STARTS[ring][0]]
@@ -264,7 +264,7 @@
      x, d, x1, a, saved, heads, w_qkv, w_out_all, b, pre, d_hid, u, d_pre, d_heads, probs, d_scores, d_qkv,
      dw_qkv, dw_out, dw_up, dw_down, dg_attn, dg_mlp,
      seg, x_sem, d_sem, out_sem, dtok_sem, heads_send, heads_recv, wout_send, wout_recv) = refs[:47]
-    ring_db, ring_p2, ring_da = [RingSum(size, *refs[47 + 7 * n:54 + 7 * n]) for n in range(3)]
+    ring_mlp, ring_da = [RingSum(size, *refs[47 + 7 * n:54 + 7 * n]) for n in range(2)]
     count = tok_hbm.shape[0]
     block_rows, hidden = x.shape[2], x.shape[3]
     rows = BLOCKS * block_rows
@@ -273,6 +273,7 @@
     scale = head_dim ** -0.5
     masks = head_masks(width, head_dim)
     me = lax.axis_index('model')
+    db_rows, p2_rows = slice(0, block_rows), slice(block_rows, 2 * block_rows)
     my_lanes = pl.ds(pl.multiple_of(me * width, width), width)
     gain_attn, gain_mlp = gains.at[0:1], gains.at[1:2]
 
@@ -301,7 +302,7 @@
 
     def out_copy(s):
         slot = lax.rem(s, SLOTS)
-        return pltpu.make_async_copy(ring_p2.whole.at[slot], out_hbm.at[s], out_sem.at[slot])
+        return pltpu.make_async_copy(ring_mlp.whole.at[slot, :, pl.ds(block_rows, block_rows)], out_hbm.at[s], out_sem.at[slot])
 
     def dtok_copy(s):
         slot = lax.rem(s, SLOTS)
@@ -321,7 +322,8 @@
         slot, x1_slot = lax.rem(s, SLOTS), lax.rem(s, plan.x1_slots)
 
         def block(r):
-            ring_p2.whole[slot, r] = (x1[x1_slot, r].astype(F32) + ring_p2.whole[slot, r].astype(F32)).astype(BF16)
+            total = x1[x1_slot, r].astype(F32) + ring_mlp.whole[slot, r, p2_rows].astype(F32)
+            ring_mlp.whole[slot, r, p2_rows] = total.astype(BF16)
         loop(BLOCKS, block)
         out_copy(s).start()
 
@@ -335,8 +337,8 @@
         loop(BLOCKS, block)
         dtok_copy(s).start()
 
-    def store_part(ring, slot, h, value):
-        ring.part[slot, h * HALF:(h + 1) * HALF] = value.astype(BF16).reshape(HALF, block_rows, hidden)
+    def store_part(ring, slot, h, value, at=slice(None)):
+        ring.part[slot, h * HALF:(h + 1) * HALF, at] = value.astype(BF16).reshape(HALF, block_rows, hidden)
 
     def norm_in(h, s):
         x_slot, slot = lax.rem(s, plan.x_slots), lax.rem(s, plan.a_slots)
@@ -403,16 +405,15 @@
 
     def grad_b(s):
         for h in range(2):
-            store_part(ring_db, lax.rem(s, SLOTS), h, mt(d_pre[h * half:(h + 1) * half], w_up[...]))
-        ring_db.stage(0, s)
+            store_part(ring_mlp, lax.rem(s, SLOTS), h, mt(d_pre[h * half:(h + 1) * half], w_up[...]), db_rows)
 
     def down(s):
         @pl.when(s >= SLOTS)
         def _():
             out_copy(s - SLOTS).wait()
         for h in range(2):
-            store_part(ring_p2, lax.rem(s, SLOTS), h, mm(u[h * half:(h + 1) * half], w_down[...]))
-        ring_p2.stage(0, s)
+            store_part(ring_mlp, lax.rem(s, SLOTS), h, mm(u[h * half:(h + 1) * half], w_down[...]), p2_rows)
+        ring_mlp.stage(0, s)
 
     def grad_up(s):
         dw_up[...] += tm(b[...].reshape(rows, hidden), d_pre[...])
@@ -425,7 +426,7 @@
 
         def block(i):
             r = h * HALF + i
-            dx, dg = norm_back(x1[x1_slot, r].astype(F32), gain_mlp[...], ring_db.whole[slot, r].astype(F32))
+            dx, dg = norm_back(x1[x1_slot, r].astype(F32), gain_mlp[...], ring_mlp.whole[slot, r, db_rows].astype(F32))
             dg_mlp[...] += rows_sum(dg)
             d[d_slot, r] = (d[d_slot, r].astype(F32) + dx).astype(BF16)
         loop(HALF, block)
@@ -486,7 +487,7 @@
     first = plan.start['p1']
     progress = make_progress(plan.points, [(gather_wout, 1, 0, 0, [first + 1, first + 4, first + 7], None)] + [
         (ring, count, plan.ring_lead(name), plan.start[name], STAGES[name], consume) for name, ring, consume in (
-            ('p1', gather_p1, consume_p1), ('db', ring_db, None), ('p2', ring_p2, consume_p2), ('da', ring_da, consume_da))])
+            ('p1', gather_p1, consume_p1), ('mlp', ring_mlp, consume_p2), ('da', ring_da, consume_da))])
 
     x_in(0).start()
     for s in range(count):
@@ -631,8 +632,8 @@
             ((8, hidden), F32), ((8, hidden), F32), ((count, 1, seq_len), jnp.int32))]
         scratch += [dma((plan.x_slots,)), dma((plan.d_slots,)), dma((SLOTS,)), dma((SLOTS,))]
         scratch += [dma((plan.head_slots, 8))] * 2 + [dma((1, 8))] * 2
-        for _ in range(3):
-            scratch += ring_buffers(block_rows, hidden) + ring_sems()
+        for ring_rows in (2 * block_rows, block_rows):
+            scratch += ring_buffers(ring_rows, hidden) + ring_sems()
         results = run_kernel(
             functools.partial(layer_kernel, size, head_dim, plan), 1, outs, [False] * 2 + [True] * 5,
             [x, d, seg_ids, gains, wqkv, wout, w_up, w_down], [False] * 2 + [True] * 6, scratch)

time: 379 us -> 381 us (level)
  no operation moved by 1% of the time
where the time goes in v4:
time: 381 us
  Pallas kernels  377 us (99%)
    pallas_call x1, Pallas kernels, run_kernel(): pl.pallas_call(kernel, out_shape=[jax.ShapeDtypeStruct(s, t) for s, t in...  364 us
    pallas_call x1, Pallas kernels, publish(): pl.pallas_call(functools.partial(publish_kernel, split), out_shape=[jax.S...  12.8 us

profile of v4, /device:TPU:81, one launch (start us, length us, event | category | flops | bytes accessed | tf_op | source)
XLA Modules:
  0.0 380.7 jit_solution(10108675417803938313)
XLA Ops:
  0.6 0.7 stack.9
  1.3 0.7 stack.10
  2.0 0.6 maximum_convert_fusion.refs_3_
  2.6 363.9 %layer_part_1.1 = (bf16[8,16,32,1024]{3,2,1,0:T(8,128)(2,1)}, bf16[8,16,32,1024]{3,2,1,0:T(8,128)(2,1)}, bf16[2,3,64,1024]{3,2,1,0:T(8,128)(2,1)}, bf16[128,1024...) custom-call(bf16[8,16,32,1024]{3,2,1,0:T(8,128)(2,1)} %bitcast.10, ...), custom_call_target="tpu_custom_call" | custom-call | tf_op jit(solution)/shard_map/layer_part_1/pallas_call | solution.py:592
  366.5 12.8 %publish.1 = (bf16[8,16,32,1024]{3,2,1,0:T(8,128)(2,1)}, bf16[8,16,32,1024]{3,2,1,0:T(8,128)(2,1)}, bf16[2,3,64,1024]{3,2,1,0:T(8,128)(2,1)}, bf16[128,1024]{1,0...) custom-call(bf16[8,16,32,1024]{3,2,1,0:T(8,128)(2,1)} %get-tuple-element.22.refs_0_, ...), custom_call_target="tpu_custom_call" | custom-call | tf_op jit(solution)/shard_map/publish/pallas_call | solution.py:564
  379.4 1.4 fusion

commit v5 on v3

--- a/solution.py
+++ b/solution.py
@@ -93,6 +93,7 @@
 
     def __init__(self, size, part, pair_in, relay_in, ring_in, whole, send, recv):
         self.part, self.pair_in, self.relay_in, self.ring_in, self.whole = part, pair_in, relay_in, ring_in, whole
+        self.finish = None
         super().__init__(size, SLOTS, self.block_view, send, recv)
 
     def block_view(self, slot, core, chip, part):
@@ -152,7 +153,9 @@
             self.sum_copy(12, s).wait_recv()
             for i in range(PIECE):
                 block = self.base(0) + i
-                self.whole[slot, block] = self.add(slot, block, [self.ring_in[slot, 0, i], self.ring_in[slot, 1, i]])
+                total = self.part[slot, block].astype(F32)
+                total = total + self.ring_in[slot, 0, i].astype(F32) + self.ring_in[slot, 1, i].astype(F32)
+                self.whole[slot, block] = self.finish(s, block, i, total).astype(BF16)
             self.gather_stage(0, s)
         else:
             self.gather_stage(j - 3, s)
@@ -164,9 +167,9 @@
 def enter(size):
     me = lax.axis_index('model')
     barrier = pltpu.get_barrier_semaphore()
-    for other in (lax.rem(me + 2, size), lax.rem(me + size - 2, size), me + 1 - 2 * lax.rem(me, 2)):
-        pl.semaphore_signal(barrier, inc=1, device_id={'model': other}, device_id_type=MESH)
-    pl.semaphore_wait(barrier, 3)
+    for step in range(1, size):
+        pl.semaphore_signal(barrier, inc=1, device_id={'model': lax.rem(me + step, size)}, device_id_type=MESH)
+    pl.semaphore_wait(barrier, size - 1)
 
 
 def make_progress(points, sums):
@@ -223,10 +226,10 @@
 
 Q_ROWS = 128
 
-ORDER = ['A0', 'A1', 'A2', 'B0', 'B1', 'A3', 'B2', 'B3', 'B4', 'B5', 'B6', 'C0', 'C1', 'C2', 'B7', 'C3', 'C4', 'C5',
-         'C6', 'C7', 'B8', 'C8']
-STAGES = {'p1': [7, 18, 19], 'db': [1, 6, 12, 16, 22, 23], 'p2': [7, 13, 20, 31, 34, 35], 'da': [1, 7, 17, 25, 31, 32]}
-STARTS = {'p1': 'A3', 'db': 'B5', 'p2': 'B6', 'da': 'C7'}
+ORDER = ['B0', 'B1', 'B2', 'B3', 'B4', 'B5', 'B6', 'C0', 'A0', 'C1', 'A1', 'C2', 'A2', 'C3', 'C4', 'A3', 'B7', 'C5',
+         'B8', 'C6']
+STAGES = {'p1': [10, 17, 23], 'db': [2, 5, 9, 13, 19, 21], 'p2': [2, 6, 14, 23, 33, 35], 'da': [2, 7, 19, 23, 35, 36]}
+STARTS = {'p1': 'A3', 'db': 'B5', 'p2': 'B6', 'da': 'C5'}
 
 
 class Plan:
@@ -237,21 +240,26 @@
         self.lead = {'A': 0}
         self.lead['B'] = self.after('p1', 'B0')
         self.lead['C'] = self.after('db', 'C0')
-        end = {ring: self.end(ring) // n for ring in STAGES}
+        end = {ring: self.step_of(ring, -1) for ring in STAGES}
+        own = {ring: self.step_of(ring, 2) for ring in STAGES}
         self.steps = max(end.values())
-        self.x_slots = end['da'] + 2
-        self.d_slots = end['da'] - self.lead['B'] + 1
-        self.x1_slots = max(self.lead['C'], end['p2']) - end['p1'] + 1
+        self.x_slots = own['da'] + 2
+        self.d_slots = max(own['db'], self.lead['B']) - self.lead['B'] + 1
+        self.x1_slots = max(own['db'], own['p2']) - end['p1'] + 1
+        self.own_slots = own['da'] - own['db'] + 1
         self.a_slots = self.lead['C'] + 1
         self.head_slots = 2 if STAGES['p1'][-1] < n else 3
         assert all(o[-1] < 2 * n for o in STAGES.values())
-        assert self.lead['C'] * n + self.pos['C1'] < (self.lead['B'] + 2) * n + self.start['db']
+        assert self.lead['C'] * n + self.pos['C0'] < (self.lead['B'] + 2) * n + self.start['db']
 
     def ring_lead(self, ring):
         return self.lead[STARTS[ring][0]]
 
-    def end(self, ring):
-        return self.ring_lead(ring) * self.points + self.start[ring] + STAGES[ring][-1]
+    def end(self, ring, stage=-1):
+        return self.ring_lead(ring) * self.points + self.start[ring] + STAGES[ring][stage]
+
+    def step_of(self, ring, stage):
+        return self.end(ring, stage) // self.points
 
     def after(self, ring, tag):
         end = self.end(ring)
@@ -263,8 +271,9 @@
      out_hbm, dtok_hbm, dw_qkv_out, dw_out_out, dw_up_out, dw_down_out, dg_out,
      x, d, x1, a, saved, heads, w_qkv, w_out_all, b, pre, d_hid, u, d_pre, d_heads, probs, d_scores, d_qkv,
      dw_qkv, dw_out, dw_up, dw_down, dg_attn, dg_mlp,
-     seg, x_sem, d_sem, out_sem, dtok_sem, heads_send, heads_recv, wout_send, wout_recv) = refs[:47]
-    ring_db, ring_p2, ring_da = [RingSum(size, *refs[47 + 7 * n:54 + 7 * n]) for n in range(3)]
+     seg, own, dg_parts, x_sem, d_sem, out_sem, dtok_sem, heads_send, heads_recv, wout_send, wout_recv,
+     dg_send, dg_recv) = refs[:51]
+    ring_db, ring_p2, ring_da = [RingSum(size, *refs[51 + 7 * n:58 + 7 * n]) for n in range(3)]
     count = tok_hbm.shape[0]
     block_rows, hidden = x.shape[2], x.shape[3]
     rows = BLOCKS * block_rows
@@ -317,22 +326,28 @@
             proj = mm(heads[h_slot, h * half:(h + 1) * half], w_out_all[...]).astype(BF16).reshape(HALF, block_rows, hidden)
             x1[x1_slot, blocks] = (x[x_slot, blocks].astype(F32) + proj.astype(F32)).astype(BF16)
 
+    def finish_db(s, block, i, total):
+        x1_slot, d_slot = lax.rem(s, plan.x1_slots), lax.rem(s, plan.d_slots)
+        dx, dg = norm_back(x1[x1_slot, block].astype(F32), gain_mlp[...], total)
+        dg_mlp[...] += rows_sum(dg)
+        d_resid = (d[d_slot, block].astype(F32) + dx).astype(BF16)
+        own[lax.rem(s, plan.own_slots), i] = d_resid
+        return d_resid
+
+    def finish_p2(s, block, i, total):
+        return x1[lax.rem(s, plan.x1_slots), block].astype(F32) + total.astype(BF16).astype(F32)
+
+    def finish_da(s, block, i, total):
+        dx, dg = norm_back(x[lax.rem(s, plan.x_slots), block].astype(F32), gain_attn[...], total)
+        dg_attn[...] += rows_sum(dg)
+        return own[lax.rem(s, plan.own_slots), i].astype(F32) + dx
+
+    ring_db.finish, ring_p2.finish, ring_da.finish = finish_db, finish_p2, finish_da
+
     def consume_p2(s):
-        slot, x1_slot = lax.rem(s, SLOTS), lax.rem(s, plan.x1_slots)
-
-        def block(r):
-            ring_p2.whole[slot, r] = (x1[x1_slot, r].astype(F32) + ring_p2.whole[slot, r].astype(F32)).astype(BF16)
-        loop(BLOCKS, block)
         out_copy(s).start()
 
     def consume_da(s):
-        slot, x_slot, d_slot = lax.rem(s, SLOTS), lax.rem(s, plan.x_slots), lax.rem(s, plan.d_slots)
-
-        def block(r):
-            dx, dg = norm_back(x[x_slot, r].astype(F32), gain_attn[...], ring_da.whole[slot, r].astype(F32))
-            dg_attn[...] += rows_sum(dg)
-            ring_da.whole[slot, r] = (d[d_slot, r].astype(F32) + dx).astype(BF16)
-        loop(BLOCKS, block)
         dtok_copy(s).start()
 
     def store_part(ring, slot, h, value):
@@ -420,18 +435,8 @@
     def grad_down(s):
         dw_down[...] += tm(u[...], d[lax.rem(s, plan.d_slots)].reshape(rows, hidden))
 
-    def grad_mid(h, s):
-        slot, x1_slot, d_slot = lax.rem(s, SLOTS), lax.rem(s, plan.x1_slots), lax.rem(s, plan.d_slots)
-
-        def block(i):
-            r = h * HALF + i
-            dx, dg = norm_back(x1[x1_slot, r].astype(F32), gain_mlp[...], ring_db.whole[slot, r].astype(F32))
-            dg_mlp[...] += rows_sum(dg)
-            d[d_slot, r] = (d[d_slot, r].astype(F32) + dx).astype(BF16)
-        loop(HALF, block)
-
     def grad_heads(s):
-        d_rows = d[lax.rem(s, plan.d_slots)].reshape(rows, hidden)
+        d_rows = ring_db.whole[lax.rem(s, SLOTS)].reshape(rows, hidden)
         d_heads[...] = mt(d_rows, w_out[...]).astype(BF16)
         dw_out[...] += tm(saved[lax.rem(s, plan.a_slots), :, 3 * width:4 * width], d_rows)
 
@@ -480,7 +485,7 @@
     work = {'A': [with_h(norm_in, 0), with_h(norm_in, 1), with_h(attend, 0), with_h(attend, 1)],
             'B': [with_h(norm_mid, 0), with_h(norm_mid, 1), up, with_h(gelu_both, 0), with_h(gelu_both, 1), grad_b, down,
                   grad_up, grad_down],
-            'C': [with_h(grad_mid, 0), with_h(grad_mid, 1), grad_heads, with_h(attend_back, 0), with_h(head_grads, 0),
+            'C': [grad_heads, with_h(attend_back, 0), with_h(head_grads, 0),
                   with_h(attend_back, 1), with_h(head_grads, 1), grad_a, grad_qkv]}
     assert sum(len(v) for v in work.values()) == plan.points
     first = plan.start['p1']
@@ -519,14 +524,27 @@
             progress(t, i)
 
     loop(count + plan.steps, step)
+    dg_parts[me, 0:1] = jnp.sum(dg_attn[...], axis=0, keepdims=True)
+    dg_parts[me, 1:2] = jnp.sum(dg_mlp[...], axis=0, keepdims=True)
+
+    def dg_copy(step, owner):
+        return pltpu.make_async_remote_copy(
+            src_ref=dg_parts.at[owner], dst_ref=dg_parts.at[owner], send_sem=dg_send.at[step], recv_sem=dg_recv.at[step],
+            device_id={'model': lax.rem(me + step, size)}, device_id_type=MESH)
+
+    for step_ahead in range(1, size):
+        dg_copy(step_ahead, me).start()
     for acc, out in ((dw_out, dw_out_out), (dw_up, dw_up_out), (dw_down, dw_down_out)):
         out[...] = acc[...].astype(BF16)
     for n in range(w_qkv_in.shape[0]):
         for j in range(3):
             at = (j * w_qkv_in.shape[0] + n) * head_dim
             dw_qkv_out[n, j] = dw_qkv[at:at + head_dim].astype(BF16)
-    dg_out[0:1] = jnp.sum(dg_attn[...], axis=0, keepdims=True)
-    dg_out[1:2] = jnp.sum(dg_mlp[...], axis=0, keepdims=True)
+    for step_ahead in range(1, size):
+        dg_copy(step_ahead, lax.rem(me + size - step_ahead, size)).wait_recv()
+    dg_out[...] = sum(dg_parts[owner] for owner in range(size))
+    for step_ahead in range(1, size):
+        dg_copy(step_ahead, me).wait_send()
     for s in range(count - SLOTS, count):
         out_copy(s).wait()
         dtok_copy(s).wait()
@@ -628,9 +646,10 @@
             ((seq_len, inner), BF16), ((seq_len, inner), BF16), ((seq_len, width), BF16),
             ((seq_len, seq_len), BF16), ((seq_len, seq_len), BF16), ((seq_len, 3 * width), BF16),
             ((3 * width, hidden), F32), ((width, hidden), F32), ((hidden, inner), F32), ((inner, hidden), F32),
-            ((8, hidden), F32), ((8, hidden), F32), ((count, 1, seq_len), jnp.int32))]
+            ((8, hidden), F32), ((8, hidden), F32), ((count, 1, seq_len), jnp.int32),
+            ((plan.own_slots, PIECE, block_rows, hidden), BF16), ((size, 2, hidden), F32))]
         scratch += [dma((plan.x_slots,)), dma((plan.d_slots,)), dma((SLOTS,)), dma((SLOTS,))]
-        scratch += [dma((plan.head_slots, 8))] * 2 + [dma((1, 8))] * 2
+        scratch += [dma((plan.head_slots, 8))] * 2 + [dma((1, 8))] * 2 + [dma((size,))] * 2
         for _ in range(3):
             scratch += ring_buffers(block_rows, hidden) + ring_sems()
         results = run_kernel(

time: 379 us -> 318 us (0.84)
  Pallas kernels: 375 us -> 314 us
    pallas_call x1, Pallas kernels: 362 us -> 301 us  [run_kernel(): pl.pallas_call(kernel, out_shape=[jax.ShapeDtypeStruct(s, t) for s, t in...]
where the time goes in v5:
time: 318 us
  Pallas kernels  314 us (99%)
    pallas_call x1, Pallas kernels, run_kernel(): pl.pallas_call(kernel, out_shape=[jax.ShapeDtypeStruct(s, t) for s, t in...  301 us
    pallas_call x1, Pallas kernels, publish(): pl.pallas_call(functools.partial(publish_kernel, split), out_shape=[jax.S...  12.8 us

profile of v5, /device:TPU:81, one launch (start us, length us, event | category | flops | bytes accessed | tf_op | source)
XLA Modules:
  0.0 318.0 jit_solution(16601257949754639669)
XLA Ops:
  0.6 0.7 stack.9
  1.3 0.7 stack.10
  2.0 0.6 maximum_convert_fusion.refs_3_
  2.6 301.2 %layer_part_1.1 = (bf16[8,16,32,1024]{3,2,1,0:T(8,128)(2,1)}, bf16[8,16,32,1024]{3,2,1,0:T(8,128)(2,1)}, bf16[2,3,64,1024]{3,2,1,0:T(8,128)(2,1)}, bf16[128,1024...) custom-call(bf16[8,16,32,1024]{3,2,1,0:T(8,128)(2,1)} %bitcast.10, ...), custom_call_target="tpu_custom_call" | custom-call | tf_op jit(solution)/shard_map/layer_part_1/pallas_call | solution.py:609
  303.8 12.8 %publish.1 = (bf16[8,16,32,1024]{3,2,1,0:T(8,128)(2,1)}, bf16[8,16,32,1024]{3,2,1,0:T(8,128)(2,1)}, bf16[2,3,64,1024]{3,2,1,0:T(8,128)(2,1)}, bf16[128,1024]{1,0...) custom-call(bf16[8,16,32,1024]{3,2,1,0:T(8,128)(2,1)} %get-tuple-element.22.refs_0_, ...), custom_call_target="tpu_custom_call" | custom-call | tf_op jit(solution)/shard_map/publish/pallas_call | solution.py:581
  316.6 1.4 fusion

commit v6 on v5

--- a/solution.py
+++ b/solution.py
@@ -30,11 +30,11 @@
     return lax.dot_general(a, b, (((0,), (0,)), ((), ())), preferred_element_type=F32)
 
 
-def loop(count, body):
+def loop(count, body, unroll=1):
     def step(i, carry):
         body(i)
         return carry
-    lax.fori_loop(0, count, step, 0)
+    lax.fori_loop(0, count, step, 0, unroll=unroll)
 
 
 class Gather:
@@ -225,6 +225,7 @@
 
 
 Q_ROWS = 128
+OUT_COLS = 256
 
 ORDER = ['B0', 'B1', 'B2', 'B3', 'B4', 'B5', 'B6', 'C0', 'A0', 'C1', 'A1', 'C2', 'A2', 'C3', 'C4', 'A3', 'B7', 'C5',
          'B8', 'C6']
@@ -323,8 +324,11 @@
         x_slot, x1_slot, h_slot = lax.rem(s, plan.x_slots), lax.rem(s, plan.x1_slots), lax.rem(s, plan.head_slots)
         for h in range(2):
             blocks = slice(h * HALF, (h + 1) * HALF)
-            proj = mm(heads[h_slot, h * half:(h + 1) * half], w_out_all[...]).astype(BF16).reshape(HALF, block_rows, hidden)
-            x1[x1_slot, blocks] = (x[x_slot, blocks].astype(F32) + proj.astype(F32)).astype(BF16)
+            for first in range(0, hidden, OUT_COLS):
+                cols = slice(first, first + OUT_COLS)
+                proj = mm(heads[h_slot, h * half:(h + 1) * half], w_out_all[:, cols]).astype(BF16)
+                proj = proj.reshape(HALF, block_rows, OUT_COLS).astype(F32)
+                x1[x1_slot, blocks, :, cols] = (x[x_slot, blocks, :, cols].astype(F32) + proj).astype(BF16)
 
     def finish_db(s, block, i, total):
         x1_slot, d_slot = lax.rem(s, plan.x1_slots), lax.rem(s, plan.d_slots)
@@ -362,7 +366,7 @@
             r = h * HALF + i
             unit, _ = norm_stats(x[x_slot, r].astype(F32))
             a[slot, r] = (unit * gain_attn[...]).astype(BF16)
-        loop(HALF, block)
+        loop(HALF, block, unroll=2)
         if h == 1:
             saved[slot, :, :3 * width] = mt(a[slot].reshape(rows, hidden), w_qkv[...]).astype(BF16)
 
@@ -384,7 +388,7 @@
             out = out.astype(BF16)
             saved[slot, part_rows, 3 * width:4 * width] = out
             heads[h_slot, part_rows, my_lanes] = out
-        loop(half // Q_ROWS, q_block)
+        loop(half // Q_ROWS, q_block, unroll=2)
         if h == 1:
             gather_p1.stage(0, s)
 
@@ -395,7 +399,7 @@
             r = h * HALF + i
             unit, _ = norm_stats(x1[x1_slot, r].astype(F32))
             b[r] = (unit * gain_mlp[...]).astype(BF16)
-        loop(HALF, block)
+        loop(HALF, block, unroll=2)
 
     def up(s):
         pre[...] = mm(b[...].reshape(rows, hidden), w_up[...])
@@ -414,7 +418,7 @@
             u[part_rows] = (0.5 * v * (1.0 + th)).astype(BF16)
             slope = 0.5 * (1.0 + th) + 0.5 * v * (1.0 - th * th) * (c * (1.0 + 3.0 * 0.044715 * v2))
             d_pre[part_rows] = (d_hid[part_rows].astype(F32) * slope).astype(BF16)
-        loop(HALF, block)
+        loop(HALF, block, unroll=2)
 
     def grad_b(s):
         for h in range(2):
@@ -456,7 +460,7 @@
                 row_dot = jnp.sum(d_p * p, axis=-1, keepdims=True)
                 probs[part_rows, :keys] = p.astype(BF16)
                 d_scores[part_rows, :keys] = (p * (d_p - row_dot) * scale).astype(BF16)
-            loop(half // Q_ROWS, q_block)
+            loop(half // Q_ROWS, q_block, unroll=2)
 
     def head_grads(head, s):
         mask = masks[head]

time: 318 us -> 303 us (0.953)
  Pallas kernels: 314 us -> 299 us
    pallas_call x1, Pallas kernels: 301 us -> 286 us  [run_kernel(): pl.pallas_call(kernel, out_shape=[jax.ShapeDtypeStruct(s, t) for s, t in...]
where the time goes in v6:
time: 303 us
  Pallas kernels  299 us (99%)
    pallas_call x1, Pallas kernels, run_kernel(): pl.pallas_call(kernel, out_shape=[jax.ShapeDtypeStruct(s, t) for s, t in...  286 us
    pallas_call x1, Pallas kernels, publish(): pl.pallas_call(functools.partial(publish_kernel, split), out_shape=[jax.S...  12.8 us

profile of v6, /device:TPU:81, one launch (start us, length us, event | category | flops | bytes accessed | tf_op | source)
XLA Modules:
  0.0 303.1 jit_solution(16732153442966837174)
XLA Ops:
  0.6 0.7 stack.9
  1.3 0.7 stack.10
  2.0 0.6 maximum_convert_fusion.refs_3_
  2.6 286.2 %layer_part_1.1 = (bf16[8,16,32,1024]{3,2,1,0:T(8,128)(2,1)}, bf16[8,16,32,1024]{3,2,1,0:T(8,128)(2,1)}, bf16[2,3,64,1024]{3,2,1,0:T(8,128)(2,1)}, bf16[128,1024...) custom-call(bf16[8,16,32,1024]{3,2,1,0:T(8,128)(2,1)} %bitcast.10, ...), custom_call_target="tpu_custom_call" | custom-call | tf_op jit(solution)/shard_map/layer_part_1/pallas_call | solution.py:613
  288.9 12.8 %publish.1 = (bf16[8,16,32,1024]{3,2,1,0:T(8,128)(2,1)}, bf16[8,16,32,1024]{3,2,1,0:T(8,128)(2,1)}, bf16[2,3,64,1024]{3,2,1,0:T(8,128)(2,1)}, bf16[128,1024]{1,0...) custom-call(bf16[8,16,32,1024]{3,2,1,0:T(8,128)(2,1)} %get-tuple-element.22.refs_0_, ...), custom_call_target="tpu_custom_call" | custom-call | tf_op jit(solution)/shard_map/publish/pallas_call | solution.py:585
  301.7 1.4 fusion

commit v7 on v6

--- a/solution.py
+++ b/solution.py
@@ -137,7 +137,7 @@
                 at = lax.rem(lax.rem(self.chip + 2, self.chips) * PIECE + i, HALF)
                 block = self.core * HALF + at
                 self.part[slot, block] = self.add(slot, block, [self.pair_in[slot, at]])
-            loop(HALF, pair)
+            loop(HALF, pair, unroll=4)
             self.sum_copy(9, s).start()
             self.sum_copy(10, s).start()
         elif j == 2:
@@ -366,7 +366,7 @@
             r = h * HALF + i
             unit, _ = norm_stats(x[x_slot, r].astype(F32))
             a[slot, r] = (unit * gain_attn[...]).astype(BF16)
-        loop(HALF, block, unroll=2)
+        loop(HALF, block, unroll=8)
         if h == 1:
             saved[slot, :, :3 * width] = mt(a[slot].reshape(rows, hidden), w_qkv[...]).astype(BF16)
 
@@ -399,7 +399,7 @@
             r = h * HALF + i
             unit, _ = norm_stats(x1[x1_slot, r].astype(F32))
             b[r] = (unit * gain_mlp[...]).astype(BF16)
-        loop(HALF, block, unroll=2)
+        loop(HALF, block, unroll=8)
 
     def up(s):
         pre[...] = mm(b[...].reshape(rows, hidden), w_up[...])
@@ -418,7 +418,7 @@
             u[part_rows] = (0.5 * v * (1.0 + th)).astype(BF16)
             slope = 0.5 * (1.0 + th) + 0.5 * v * (1.0 - th * th) * (c * (1.0 + 3.0 * 0.044715 * v2))
             d_pre[part_rows] = (d_hid[part_rows].astype(F32) * slope).astype(BF16)
-        loop(HALF, block, unroll=2)
+        loop(HALF, block, unroll=8)
 
     def grad_b(s):
         for h in range(2):

time: 303 us -> 302 us (level)
  no operation moved by 1% of the time
where the time goes in v7:
time: 302 us; the launch traced here: 301 us
  Pallas kernels  297 us (98%)
    pallas_call x1, Pallas kernels, run_kernel(): pl.pallas_call(kernel, out_shape=[jax.ShapeDtypeStruct(s, t) for s, t in...  285 us
    pallas_call x1, Pallas kernels, publish(): pl.pallas_call(functools.partial(publish_kernel, split), out_shape=[jax.S...  12.8 us

profile of v7, /device:TPU:81, one launch (start us, length us, event | category | flops | bytes accessed | tf_op | source)
XLA Modules:
  0.0 301.4 jit_solution(16965928012547994730)
XLA Ops:
  0.6 0.7 stack.9
  1.3 0.7 stack.10
  2.0 0.6 maximum_convert_fusion.refs_3_
  2.6 284.6 %layer_part_1.1 = (bf16[8,16,32,1024]{3,2,1,0:T(8,128)(2,1)}, bf16[8,16,32,1024]{3,2,1,0:T(8,128)(2,1)}, bf16[2,3,64,1024]{3,2,1,0:T(8,128)(2,1)}, bf16[128,1024...) custom-call(bf16[8,16,32,1024]{3,2,1,0:T(8,128)(2,1)} %bitcast.10, ...), custom_call_target="tpu_custom_call" | custom-call | tf_op jit(solution)/shard_map/layer_part_1/pallas_call | solution.py:613
  287.2 12.8 %publish.1 = (bf16[8,16,32,1024]{3,2,1,0:T(8,128)(2,1)}, bf16[8,16,32,1024]{3,2,1,0:T(8,128)(2,1)}, bf16[2,3,64,1024]{3,2,1,0:T(8,128)(2,1)}, bf16[128,1024]{1,0...) custom-call(bf16[8,16,32,1024]{3,2,1,0:T(8,128)(2,1)} %get-tuple-element.22.refs_0_, ...), custom_call_target="tpu_custom_call" | custom-call | tf_op jit(solution)/shard_map/publish/pallas_call | solution.py:585
  300.0 1.4 fusion
